TPU v7x, 256 devices: a whole 4x4x8 slice. The times are simulated.
256 devices in a mesh: mem: 32 (over x, y, core), mp: 8 (over z).
Axes of the slice: x: 4, y: 4, z: 8, core: 2. Of those that a mesh axis runs over, the one named last changes fastest.
Arguments:
- queries: bfloat16 [12288, 4096], P('mem', 'mp'), may hold values from -5 to 5
- local_keys: bfloat16 [12288, 4096], P('mem', 'mp'), may hold values from -5 to 5
- local_values: bfloat16 [12288, 4096], P('mem', 'mp'), may hold values from -6 to 6
- memory_keys: bfloat16 [65536, 4096], P('mem', 'mp'), may hold values from -5 to 5
- memory_values: bfloat16 [65536, 4096], P('mem', 'mp'), may hold values from -6 to 6
- grad_out: bfloat16 [12288, 4096], P('mem'), may hold values from -6 to 6
- out_weight: bfloat16 [4096, 4096], P('mem', 'mp'), may hold values from -0.09375 to 0.09375
- gate_logits: float32 [32], P('mp'), may hold values from -2 to 2
- tile_ids: int32 [96, 32, 4], P('mem', 'mp'), may hold values from 0 to 511, as said below
- window: int32 [96], P('mem'), may hold values from 1 to 256, as said below
Outputs:
- grad_queries: bfloat16 [12288, 4096], P('mem', 'mp')
- grad_keys: bfloat16 [12288, 4096], P('mem', 'mp')
- grad_values: bfloat16 [12288, 4096], P('mem', 'mp')
Inputs may be any that keep to these rules, and one draw needn't show every extreme that they name: `tile_ids`: owner of tile id t is t // 16. Among the 48 ids of the blocks and heads that one device holds (one index of mem and of mp), at most 3 name tiles of any one owner; in every draw one owner receives exactly 3 of them from every device. Ids of one block and head may repeat. `window`: 256 is taken by some block in every draw.
All inputs are finite; a program needn't handle non-finite values.
Results may differ from a plain program's by a relative error of at most 0.011.
Values may be sent and summed in bfloat16 or wider, within the bound.
No kernel may reach another device: no remote copies, remote signals or barrier semaphores. Data moves between devices by JAX's collectives and lax.ppermute only.
A program may use at most 128 MiB of HBM per device.

v0:
```python
import math

import jax
import jax.numpy as jnp
from jax import lax
from jax.sharding import PartitionSpec as P


def shifted(x, axis, by):
    devices = lax.axis_size(axis)
    pairs = [(i, i + by) for i in range(devices) if 0 <= i + by < devices]
    return lax.ppermute(x, axis, pairs)


def head_major(rows, local_head_count, head_features, block_count, rows_per_block):
    return (
        rows.reshape(rows.shape[0], local_head_count, head_features)
        .transpose(1, 0, 2)
        .reshape(local_head_count, block_count, rows_per_block, head_features)
    )


def spread_blocks(parts):
    total = jnp.pad(parts[0], ((0, 0), (0, 2), (0, 0), (0, 0)))
    total = total + jnp.pad(parts[1], ((0, 0), (1, 1), (0, 0), (0, 0)))
    total = total + jnp.pad(parts[2], ((0, 0), (2, 0), (0, 0), (0, 0)))
    return total


def token_major(blocks16):
    heads_here, block_count, rows_per_block, head_features = blocks16.shape
    return blocks16.transpose(1, 2, 0, 3).reshape(
        block_count * rows_per_block, heads_here * head_features
    )


def body(
    queries,
    local_keys,
    local_values,
    memory_keys,
    memory_values,
    grad_out,
    out_weight,
    gate_logits,
    tile_ids,
    window,
):
    tokens_here = queries.shape[0]
    width = queries.shape[1]
    local_head_count = gate_logits.shape[0]
    head_features = width // local_head_count
    block_list = tile_ids.shape[0]
    nearest_count = tile_ids.shape[2]
    rows_per_block = tokens_here // block_list
    tiles_here = memory_keys.shape[0] // rows_per_block
    tile_holders = lax.axis_size("mem")
    retrieved_tiles = block_list * local_head_count * nearest_count
    memory_slots = min(retrieved_tiles, max(2, 2 * retrieved_tiles // tile_holders))
    score_scale = 1.0 / math.sqrt(head_features)
    head_grad = jnp.dot(
        grad_out,
        lax.all_gather(out_weight, "mem", axis=0, tiled=True),
        preferred_element_type=jnp.float32,
    )
    head_grad_hm = head_major(
        head_grad, local_head_count, head_features, block_list, rows_per_block
    )
    gate_heads = jax.nn.sigmoid(gate_logits)[:, None, None, None]
    grad_memory = (gate_heads * head_grad_hm).astype(jnp.bfloat16)
    grad_local = ((1.0 - gate_heads) * head_grad_hm).astype(jnp.bfloat16)
    query_hm = head_major(queries, local_head_count, head_features, block_list, rows_per_block)
    flat_ids = tile_ids.reshape(-1)
    owner = flat_ids // tiles_here
    local_tile = flat_ids % tiles_here
    head_of = jnp.broadcast_to(
        jnp.arange(local_head_count, dtype=jnp.int32)[None, :, None], tile_ids.shape
    ).reshape(-1)
    codes_flat = local_tile * local_head_count + head_of
    onehot = (owner[:, None] == jnp.arange(tile_holders, dtype=jnp.int32)[None, :]).astype(
        jnp.int32
    )
    earlier = jnp.cumsum(onehot, axis=0) - onehot
    position = jnp.sum(earlier * onehot, axis=1)
    slot = owner * memory_slots + position
    slot_ordered = slot.reshape(tile_ids.shape).transpose(1, 0, 2).reshape(-1)
    request = (
        jnp.zeros((tile_holders * memory_slots,), jnp.int32)
        .at[slot]
        .set(codes_flat)
        .reshape(tile_holders, memory_slots)
    )
    mem_key4 = memory_keys.reshape(tiles_here, rows_per_block, local_head_count, head_features)
    mem_val4 = memory_values.reshape(tiles_here, rows_per_block, local_head_count, head_features)

    def regroup(array):
        flat = array.reshape((tile_holders * memory_slots,) + array.shape[2:])[slot_ordered]
        return flat.reshape((local_head_count, block_list, nearest_count) + array.shape[2:])

    codes = lax.all_to_all(request, "mem", split_axis=0, concat_axis=0, tiled=True)
    tile_part = codes // local_head_count
    head_part = codes % local_head_count
    tile_keys = mem_key4[tile_part, :, head_part, :]
    tile_values = mem_val4[tile_part, :, head_part, :]
    keys_mem = regroup(
        lax.all_to_all(tile_keys, "mem", split_axis=0, concat_axis=0, tiled=True)
    ).reshape(local_head_count, block_list, nearest_count * rows_per_block, head_features)
    vals_mem = regroup(
        lax.all_to_all(tile_values, "mem", split_axis=0, concat_axis=0, tiled=True)
    ).reshape(local_head_count, block_list, nearest_count * rows_per_block, head_features)
    scores = (
        jnp.einsum("hbqd,hbkd->hbqk", query_hm, keys_mem, preferred_element_type=jnp.float32)
        * score_scale
    )
    probs = jax.nn.softmax(scores, axis=-1)
    dprobs = jnp.einsum(
        "hbqd,hbkd->hbqk", grad_memory, vals_mem, preferred_element_type=jnp.float32
    )
    delta = jnp.sum(probs * dprobs, axis=-1, keepdims=True)
    dscores = probs * (dprobs - delta)
    memory_qgrad = (
        jnp.einsum("hbqk,hbkd->hbqd", dscores, keys_mem.astype(jnp.float32)) * score_scale
    )
    halo_keys, halo_values = shifted(
        (
            local_keys[tokens_here - 2 * rows_per_block :],
            local_values[tokens_here - 2 * rows_per_block :],
        ),
        "mem",
        1,
    )
    key_hm = head_major(
        jnp.concatenate([halo_keys, local_keys], axis=0),
        local_head_count,
        head_features,
        block_list + 2,
        rows_per_block,
    )
    value_hm = head_major(
        jnp.concatenate([halo_values, local_values], axis=0),
        local_head_count,
        head_features,
        block_list + 2,
        rows_per_block,
    )
    offset = lax.axis_index("mem") * tokens_here
    query_pos = (
        offset
        + jnp.arange(block_list, dtype=jnp.int32)[:, None] * rows_per_block
        + jnp.arange(rows_per_block, dtype=jnp.int32)[None, :]
    )
    key_pos = (
        query_pos[:, :1, None]
        - 2 * rows_per_block
        + jnp.arange(3, dtype=jnp.int32)[None, :, None] * rows_per_block
        + jnp.arange(rows_per_block, dtype=jnp.int32)[None, None, :]
    )
    later_pos = key_pos[:, None]
    query_here = query_pos[:, :, None, None]
    allowed = (
        (later_pos <= query_here)
        & (later_pos > query_here - window[:, None, None, None])
        & (later_pos >= 0)
    )
    score_parts = [
        jnp.einsum(
            "hbqd,hbkd->hbqk",
            query_hm,
            key_hm[:, step : step + block_list],
            preferred_element_type=jnp.float32,
        )
        for step in range(3)
    ]
    scores = jnp.stack(score_parts, axis=3) * score_scale
    scores = jnp.where(allowed[None], scores, -jnp.inf)
    row_peak = jnp.max(scores, axis=(3, 4), keepdims=True)
    expo = jnp.exp(scores - row_peak)
    probs = expo / jnp.sum(expo, axis=(3, 4), keepdims=True)
    probs16 = probs.astype(jnp.bfloat16)
    dprob_parts = [
        jnp.einsum(
            "hbqd,hbkd->hbqk",
            grad_local,
            value_hm[:, step : step + block_list],
            preferred_element_type=jnp.float32,
        )
        for step in range(3)
    ]
    dprobs = jnp.stack(dprob_parts, axis=3)
    delta_local = jnp.sum(probs * dprobs, axis=(3, 4), keepdims=True)
    dscores16 = (probs * (dprobs - delta_local)).astype(jnp.bfloat16)
    local_qgrad = jnp.einsum(
        "hbqk,hbkd->hbqd",
        dscores16[:, :, :, 0],
        key_hm[:, 0:block_list],
        preferred_element_type=jnp.float32,
    )
    local_qgrad = local_qgrad + jnp.einsum(
        "hbqk,hbkd->hbqd",
        dscores16[:, :, :, 1],
        key_hm[:, 1 : block_list + 1],
        preferred_element_type=jnp.float32,
    )
    local_qgrad = local_qgrad + jnp.einsum(
        "hbqk,hbkd->hbqd",
        dscores16[:, :, :, 2],
        key_hm[:, 2 : block_list + 2],
        preferred_element_type=jnp.float32,
    )
    local_qgrad = local_qgrad * score_scale
    key_parts = [
        jnp.einsum(
            "hbqk,hbqd->hbkd",
            dscores16[:, :, :, step],
            query_hm,
            preferred_element_type=jnp.float32,
        )
        * score_scale
        for step in range(3)
    ]
    value_parts = [
        jnp.einsum(
            "hbqk,hbqd->hbkd",
            probs16[:, :, :, step],
            grad_local,
            preferred_element_type=jnp.float32,
        )
        for step in range(3)
    ]
    key_all = spread_blocks(key_parts)
    value_all = spread_blocks(value_parts)
    back_keys, back_values = shifted((key_all[:, :2], value_all[:, :2]), "mem", -1)
    key_own = key_all[:, 2:]
    value_own = value_all[:, 2:]
    grad_keys = jnp.concatenate(
        [key_own[:, : block_list - 2], key_own[:, block_list - 2 :] + back_keys], axis=1
    )
    grad_values = jnp.concatenate(
        [value_own[:, : block_list - 2], value_own[:, block_list - 2 :] + back_values], axis=1
    )
    grad_queries = (memory_qgrad + local_qgrad).astype(jnp.bfloat16)
    return (
        token_major(grad_queries),
        token_major(grad_keys.astype(jnp.bfloat16)),
        token_major(grad_values.astype(jnp.bfloat16)),
    )


def solution(mesh):
    in_specs = (
        P("mem", "mp"),
        P("mem", "mp"),
        P("mem", "mp"),
        P("mem", "mp"),
        P("mem", "mp"),
        P("mem", None),
        P("mem", "mp"),
        P("mp"),
        P("mem", "mp", None),
        P("mem"),
    )
    out_specs = (P("mem", "mp"), P("mem", "mp"), P("mem", "mp"))
    return jax.shard_map(body, mesh=mesh, in_specs=in_specs, out_specs=out_specs, check_vma=False)
```

profile of v0, /device:TPU:1, one launch (start us, length us, event | category | flops | bytes accessed | tf_op | source)
XLA Modules:
  0.0 178.7 jit_solution(2363167351981583547)
XLA Ops:
  7.2 0.7 all-gather.2.cloned.1.call-update
  7.9 1.0 reshape.444
  8.9 0.8 reshape.445
  10.1 0.7 scatter_custom_fusion
  10.9 0.7 all_to_all.14
  11.6 8.6 %all-to-all-start = ((s32[32,1,3]{2,1,0:T(1,128)}), s32[32,1,3]{2,1,0:T(1,128)S(1)}, u32[]{:S(2)}, u32[]{:S(2)}) async-start(s32[32,1,3]{2,1,0:T(1,128)} %bitcast.2), calls=%async_computation | async-start | bytes 32768 | tf_op jit(solution)/shard_map/all_to_all | solution.py:100
  20.2 4.0 %reshape.498 = bf16[16,128,4,128]{3,2,1,0:T(4,128)(2,1)} reshape(bf16[2048,512]{1,0:T(8,128)(2,1)} %param.13) | data formatting | bytes 4194304 | tf_op jit(solution)/shard_map/reshape | solution.py:93
  24.2 3.5 %copy.116 = bf16[16,128,4,128]{3,1,2,0:T(8,128)(2,1)} copy(bf16[16,128,4,128]{3,2,1,0:T(4,128)(2,1)} %reshape.498) | data formatting | bytes 4194304 | tf_op jit(solution)/shard_map/reshape | solution.py:93
  28.0 4.8 %gather_fusion = bf16[96,128,128]{2,1,0:T(8,128)(2,1)} fusion(bf16[16,128,4,128]{3,1,2,0:T(8,128)(2,1)} %copy.116, s32[96]{0:T(128)S(1)} %reshape.462), kind=kCustom, calls=%fused_computation | custom fusion | bytes 6292224 | tf_op jit(solution)/shard_map/gather | solution.py:103
  32.8 7.6 %all-to-all-start.1 = ((bf16[32,3,128,128]{3,2,1,0:T(8,128)(2,1)}), bf16[32,3,128,128]{3,2,1,0:T(8,128)(2,1)}, u32[]{:S(2)}, u32[]{:S(2)}) async-start(bf16[32,3,128,128]{3,2,1,0:T(8,128)(2,1)} %bitcast.159), calls=%async_computation.1 | async-start | bytes 6291456 | tf_op jit(solution)/shard_map/all_to_all | solution.py:106
  40.3 1.7 slice.82
  42.0 3.5 %collective-permute-start.1 = (bf16[256,512]{1,0:T(8,128)(2,1)}, bf16[256,512]{1,0:T(8,128)(2,1)}, u32[]{:S(2)}, u32[]{:S(2)}) collective-permute-start(bf16[256,512]{1,0:T(8,128)(2,1)} %slice.82), channel_id=1, source_target_pairs={{0,8},{8,16},{16,24},{24,32},{32,40},{40,48},{48,56},{56,64},{64,7... | collective-permute-start | bytes 786440 | tf_op jit(solution)/shard_map/ppermute | solution.py:12
  45.6 0.7 slice.78
  46.3 2.0 %collective-permute-start = (bf16[256,512]{1,0:T(8,128)(2,1)}, bf16[256,512]{1,0:T(8,128)(2,1)}, u32[]{:S(2)}, u32[]{:S(2)}) collective-permute-start(bf16[256,512]{1,0:T(8,128)(2,1)} %slice.78), channel_id=1, source_target_pairs={{0,8},{8,16},{16,24},{24,32},{32,40},{40,48},{48,56},{56,64},{64,7... | collective-permute-start | bytes 786440 | tf_op jit(solution)/shard_map/ppermute | solution.py:12
  48.5 4.0 %reshape.499 = bf16[16,128,4,128]{3,2,1,0:T(4,128)(2,1)} reshape(bf16[2048,512]{1,0:T(8,128)(2,1)} %param.14) | data formatting | bytes 4194304 | tf_op jit(solution)/shard_map/reshape | solution.py:94
  52.5 3.5 %copy.121 = bf16[16,128,4,128]{3,1,2,0:T(8,128)(2,1)} copy(bf16[16,128,4,128]{3,2,1,0:T(4,128)(2,1)} %reshape.499) | data formatting | bytes 4194304 | tf_op jit(solution)/shard_map/reshape | solution.py:94
  56.0 4.7 %gather_fusion.2 = bf16[96,128,128]{2,1,0:T(8,128)(2,1)} fusion(bf16[16,128,4,128]{3,1,2,0:T(8,128)(2,1)} %copy.121, s32[96]{0:T(128)S(1)} %reshape.462), kind=kCustom, calls=%fused_computation.2 | custom fusion | bytes 6292224 | tf_op jit(solution)/shard_map/gather | solution.py:104
  60.7 26.3 %all-to-all-done.1 = bf16[32,3,128,128]{3,2,1,0:T(8,128)(2,1)} async-done(((bf16[32,3,128,128]{3,2,1,0:T(8,128)(2,1)}), bf16[32,3,128,128]{3,2,1,0:T(8,128)(2,1)}, u32[]{:S(2)}, u32[]{:S(2)}) %all-to-all-start.1) | async-done | bytes 3145760 | tf_op jit(solution)/shard_map/all_to_all | solution.py:106
  87.0 5.5 %all-to-all-start.2 = ((bf16[32,3,128,128]{3,2,1,0:T(8,128)(2,1)}), bf16[32,3,128,128]{3,2,1,0:T(8,128)(2,1)}, u32[]{:S(2)}, u32[]{:S(2)}) async-start(bf16[32,3,128,128]{3,2,1,0:T(8,128)(2,1)} %bitcast.158), calls=%async_computation.2 | async-start | bytes 6291456 | tf_op jit(solution)/shard_map/all_to_all | solution.py:109
  92.7 1.3 broadcast_subtract_fusion.1
  94.2 1.1 and_and_fusion
  95.3 0.8 reshape.449
  96.1 1.0 copy.118
  97.2 0.6 pad_clamp_fusion
  97.8 1.2 copy_bitcast_fusion.1
  99.0 2.3 %copy_bitcast_fusion = bf16[640,4,128]{2,0,1:T(8,128)(2,1)} fusion(bf16[384,512]{1,0:T(8,128)(2,1)} %param.12, bf16[256,512]{1,0:T(8,128)(2,1)} %collective-permute-done.1), kind=kLoop, calls=%fused_computation.45 | loop fusion | flops 1310720 | bytes 1310720 | tf_op jit(solution)/shard_map/reshape | solution.py:17
  101.2 0.4 convolution_bitcast_fusion
  101.6 0.4 convolution_bitcast_fusion.1
  102.7 0.5 fusion.11
  103.3 3.9 %gather_fusion.1 = bf16[48,128,128]{2,1,0:T(8,128)(2,1)} fusion(bf16[96,128,128]{2,1,0:T(8,128)(2,1)} %bitcast.5, s32[1024]{0:T(1024)} %pad_clamp_fusion), kind=kCustom, calls=%fused_computation.1 | custom fusion | bytes 3145920 | tf_op jit(solution)/shard_map/gather | solution.py:97
  107.3 25.1 %all-to-all-done.2 = bf16[32,3,128,128]{3,2,1,0:T(8,128)(2,1)} async-done(((bf16[32,3,128,128]{3,2,1,0:T(8,128)(2,1)}), bf16[32,3,128,128]{3,2,1,0:T(8,128)(2,1)}, u32[]{:S(2)}, u32[]{:S(2)}) %all-to-all-start.2) | async-done | bytes 3145760 | tf_op jit(solution)/shard_map/all_to_all | solution.py:109
  132.4 4.0 %gather_fusion.3 = bf16[48,128,128]{2,1,0:T(8,128)(2,1)} fusion(bf16[96,128,128]{2,1,0:T(8,128)(2,1)} %bitcast.15, s32[1024]{0:T(1024)} %pad_clamp_fusion), kind=kCustom, calls=%fused_computation.3 | custom fusion | bytes 3145920 | tf_op jit(solution)/shard_map/gather | solution.py:97
  136.4 4.9 %fusion.62 = (f32[4,3,128]{2,1,0:T(4,128)}, f32[4,3,128,512]{2,3,1,0:T(8,128)}) fusion(bf16[4,3,512,128]{3,2,1,0:T(8,128)(2,1)} %bitcast.170, bf16[4,3,128,128]{3,2,1,0:T(8,128)(2,1)S(1)} %bitcast.154), kind=kOutput, calls=%fused_computation.138 | convolution fusion | flops 203686400 | bytes 5117952 | tf_op jit(solution)/shard_map/sub | solution.py:115
  141.3 4.9 %fusion.63 = f32[384,512]{1,0:T(8,128)} fusion(bf16[384,4096]{1,0:T(8,128)(2,1)S(1)} %copy-done, bf16[4096,512]{1,0:T(8,128)(2,1)} %all-gather.2.cloned.1.call-done), kind=kOutput, calls=%fused_computation.139 | convolution fusion | flops 1610612736 | bytes 8126464 | tf_op jit(solution)/shard_map/dot_general | solution.py:61
  146.2 1.4 reshape.451
  147.8 0.9 copy-done.10
  148.7 0.4 convolution_bitcast_fusion.3
  150.3 0.7 multiply_reduce_fusion.1
  151.0 0.9 fusion.61
  154.4 2.6 %collective-permute-start.3 = (f32[4,2,128,128]{3,2,1,0:T(8,128)S(1)}, f32[4,2,128,128]{3,2,1,0:T(8,128)S(1)}, u32[]{:S(2)}, u32[]{:S(2)}) collective-permute-start(f32[4,2,128,128]{3,2,1,0:T(8,128)S(1)} %slice.123), channel_id=1, source_target_pairs={{8,0},{16,8},{24,16},{32,24},{40,32},{48,40},{56,48},{64,56},{72,6... | collective-permute-start | bytes 1572872 | tf_op jit(solution)/shard_map/ppermute | solution.py:12
  157.2 2.4 %collective-permute-start.2 = (f32[4,2,128,128]{3,2,1,0:T(8,128)S(1)}, f32[4,2,128,128]{3,2,1,0:T(8,128)S(1)}, u32[]{:S(2)}, u32[]{:S(2)}) collective-permute-start(f32[4,2,128,128]{3,2,1,0:T(8,128)S(1)} %slice.117), channel_id=1, source_target_pairs={{8,0},{16,8},{24,16},{32,24},{40,32},{48,40},{56,48},{64,56},{72,6... | collective-permute-start | bytes 1572872 | tf_op jit(solution)/shard_map/ppermute | solution.py:12
  160.4 0.7 multiply_reduce_fusion
  161.1 0.7 copy-done.13
  161.8 0.9 fusion.23
  163.0 0.8 copy.152
  163.8 1.0 collective-permute-done.3
  165.3 5.2 %collective-permute-done.2 = f32[4,2,128,128]{3,2,1,0:T(8,128)S(1)} collective-permute-done((f32[4,2,128,128]{3,2,1,0:T(8,128)S(1)}, f32[4,2,128,128]{3,2,1,0:T(8,128)S(1)}, u32[]{:S(2)}, u32[]{:S(2)}) %collective-permute-start.2) | collective-permute-done | bytes 524320 | tf_op jit(solution)/shard_map/ppermute | solution.py:12
  170.9 1.0 copy_bitcast_fusion.2
  (100 shorter events, 8.0 us)
Async XLA Ops:
  7.2 134.1 %copy-start = (bf16[384,4096]{1,0:T(8,128)(2,1)S(1)}, bf16[384,4096]{1,0:T(8,128)(2,1)}, u32[]{:S(2)}) copy-start(bf16[384,4096]{1,0:T(8,128)(2,1)} %param.15) | copy-start | bytes 9437188
  7.2 134.1 %all-gather.2.cloned.1.call-start = ((), (), s32[]{:S(2)}) async-start(), calls=%async_computation.3 | async-start | bytes 4325376 | tf_op jit(solution)/shard_map/all_gather | solution.py:63
  11.6 16.1 %all-to-all-start = ((s32[32,1,3]{2,1,0:T(1,128)}), s32[32,1,3]{2,1,0:T(1,128)S(1)}, u32[]{:S(2)}, u32[]{:S(2)}) async-start(s32[32,1,3]{2,1,0:T(1,128)} %bitcast.2), calls=%async_computation | async-start | bytes 32768 | tf_op jit(solution)/shard_map/all_to_all | solution.py:100
  32.8 12.8 %copy-start.15 = (bf16[384,512]{1,0:T(8,128)(2,1)S(1)}, bf16[384,512]{1,0:T(8,128)(2,1)}, u32[]{:S(2)}) copy-start(bf16[384,512]{1,0:T(8,128)(2,1)} %param.11) | copy-start | bytes 1179652
  32.8 15.6 %copy-start.17 = (s32[3,4,4]{2,1,0:T(4,128)S(1)}, s32[3,4,4]{2,1,0:T(4,128)}, u32[]{:S(2)}) copy-start(s32[3,4,4]{2,1,0:T(4,128)} %param.18) | copy-start | bytes 580
  32.8 54.2 %all-to-all-start.1 = ((bf16[32,3,128,128]{3,2,1,0:T(8,128)(2,1)}), bf16[32,3,128,128]{3,2,1,0:T(8,128)(2,1)}, u32[]{:S(2)}, u32[]{:S(2)}) async-start(bf16[32,3,128,128]{3,2,1,0:T(8,128)(2,1)} %bitcast.159), calls=%async_computation.1 | async-start | bytes 6291456 | tf_op jit(solution)/shard_map/all_to_all | solution.py:106
  42.0 57.0 %collective-permute-start.1 = (bf16[256,512]{1,0:T(8,128)(2,1)}, bf16[256,512]{1,0:T(8,128)(2,1)}, u32[]{:S(2)}, u32[]{:S(2)}) collective-permute-start(bf16[256,512]{1,0:T(8,128)(2,1)} %slice.82), channel_id=1, source_target_pairs={{0,8},{8,16},{16,24},{24,32},{32,40},{40,48},{48,56},{56,64},{64,7... | collective-permute-start | bytes 786440 | tf_op jit(solution)/shard_map/ppermute | solution.py:12
  46.3 51.5 %collective-permute-start = (bf16[256,512]{1,0:T(8,128)(2,1)}, bf16[256,512]{1,0:T(8,128)(2,1)}, u32[]{:S(2)}, u32[]{:S(2)}) collective-permute-start(bf16[256,512]{1,0:T(8,128)(2,1)} %slice.78), channel_id=1, source_target_pairs={{0,8},{8,16},{16,24},{24,32},{32,40},{40,48},{48,56},{56,64},{64,7... | collective-permute-start | bytes 786440 | tf_op jit(solution)/shard_map/ppermute | solution.py:12
  87.0 5.5 %copy-start.19 = (s32[3]{0:T(128)S(1)}, s32[3]{0:T(128)}, u32[]{:S(2)}) copy-start(s32[3]{0:T(128)} %param.19) | copy-start | bytes 40
  87.0 8.3 %copy-start.16 = (bf16[384,512]{1,0:T(8,128)(2,1)S(1)}, bf16[384,512]{1,0:T(8,128)(2,1)}, u32[]{:S(2)}) copy-start(bf16[384,512]{1,0:T(8,128)(2,1)} %param.10) | copy-start | bytes 1179652
  87.0 45.4 %all-to-all-start.2 = ((bf16[32,3,128,128]{3,2,1,0:T(8,128)(2,1)}), bf16[32,3,128,128]{3,2,1,0:T(8,128)(2,1)}, u32[]{:S(2)}, u32[]{:S(2)}) async-start(bf16[32,3,128,128]{3,2,1,0:T(8,128)(2,1)} %bitcast.158), calls=%async_computation.2 | async-start | bytes 6291456 | tf_op jit(solution)/shard_map/all_to_all | solution.py:109
  98.9 3.1 %copy-start.2 = (bf16[640,4,128]{2,0,1:T(8,128)(2,1)}, bf16[640,4,128]{2,0,1:T(8,128)(2,1)S(1)}, u32[]{:S(2)}) copy-start(bf16[640,4,128]{2,0,1:T(8,128)(2,1)S(1)} %copy_bitcast_fusion.1) | copy-start | bytes 1966084
  101.2 1.2 copy-start.11
  101.6 1.1 copy-start.4
  102.0 1.3 copy-start.6
  102.4 0.9 copy-start.8
  146.2 1.5 copy-start.18
  147.6 1.1 copy-start.10
  148.6 1.2 copy-start.5
  148.6 1.4 copy-start.7
  148.6 1.6 copy-start.9
  148.6 1.6 copy-start.12
  152.8 1.1 copy-start.3
  154.4 10.5 %collective-permute-start.3 = (f32[4,2,128,128]{3,2,1,0:T(8,128)S(1)}, f32[4,2,128,128]{3,2,1,0:T(8,128)S(1)}, u32[]{:S(2)}, u32[]{:S(2)}) collective-permute-start(f32[4,2,128,128]{3,2,1,0:T(8,128)S(1)} %slice.123), channel_id=1, source_target_pairs={{8,0},{16,8},{24,16},{32,24},{40,32},{48,40},{56,48},{64,56},{72,6... | collective-permute-start | bytes 1572872 | tf_op jit(solution)/shard_map/ppermute | solution.py:12
  157.1 3.2 %copy-start.22 = (f32[4,3,128]{2,1,0:T(4,128)S(1)}, f32[4,3,128]{2,1,0:T(4,128)}, u32[]{:S(2)}) copy-start(f32[4,3,128]{2,1,0:T(4,128)} %get-tuple-element.11) | copy-start | bytes 18436
  157.2 3.1 %copy-start.14 = (bf16[48,128,128]{2,1,0:T(8,128)(2,1)S(1)}, bf16[48,128,128]{2,1,0:T(8,128)(2,1)}, u32[]{:S(2)}) copy-start(bf16[48,128,128]{2,1,0:T(8,128)(2,1)} %gather_fusion.3) | copy-start | bytes 4718596
  157.2 3.1 %copy-start.20 = (f32[4]{0:T(128)S(1)}, f32[4]{0:T(128)}, u32[]{:S(2)}) copy-start(f32[4]{0:T(128)} %get-tuple-element.4) | copy-start | bytes 52
  157.2 3.1 %copy-start.21 = (f32[4,3,128,512]{2,3,1,0:T(8,128)S(1)}, f32[4,3,128,512]{2,3,1,0:T(8,128)}, u32[]{:S(2)}) copy-start(f32[4,3,128,512]{2,3,1,0:T(8,128)} %get-tuple-element.12) | copy-start | bytes 9437188
  157.2 13.2 %collective-permute-start.2 = (f32[4,2,128,128]{3,2,1,0:T(8,128)S(1)}, f32[4,2,128,128]{3,2,1,0:T(8,128)S(1)}, u32[]{:S(2)}, u32[]{:S(2)}) collective-permute-start(f32[4,2,128,128]{3,2,1,0:T(8,128)S(1)} %slice.117), channel_id=1, source_target_pairs={{8,0},{16,8},{24,16},{32,24},{40,32},{48,40},{56,48},{64,56},{72,6... | collective-permute-start | bytes 1572872 | tf_op jit(solution)/shard_map/ppermute | solution.py:12
  160.3 1.4 copy-start.13
  165.0 6.9 %copy-start.1 = (bf16[384,4096]{1,0:T(8,128)(2,1)S(1)}, bf16[384,4096]{1,0:T(8,128)(2,1)}, u32[]{:S(2)}) copy-start(bf16[384,4096]{1,0:T(8,128)(2,1)} %param.15) | copy-start | bytes 9437188
Sparse Core Ops, SparseCore 0:
  10.5 79.2 all-gather.1
where the time goes:
time: 180 us; the launch traced here: 179 us
  waiting for transfers between devices  58.3 us (32%)
  local copies, waits for them, and re-layouts  47.1 us (26%)
  starting transfers between devices  32.2 us (18%)
  matrix products  16.2 us (9%)
  between operations  14.6 us (8%)
  other arithmetic  10.4 us (6%)
    all_to_all x1, waiting for transfers between devices, body(): lax.all_to_all(tile_keys, 'mem', split_axis=0, concat_axis=0, tiled=True)  26.3 us
    all_to_all x1, waiting for transfers between devices, body(): lax.all_to_all(tile_values, 'mem', split_axis=0, concat_axis=0, tiled=True)  25.1 us
    ppermute x4, starting transfers between devices, shifted(): return lax.ppermute(x, axis, pairs)  10.5 us
    all_to_all x1, starting transfers between devices, body(): lax.all_to_all(request, 'mem', split_axis=0, concat_axis=0, tiled=True)  8.58 us
    gather x2, local copies, waits for them, and re-layouts, regroup(): array.reshape((tile_holders * memory_slots,) + array.shape[2:])  7.98 us
    all_to_all x1, starting transfers between devices, body(): lax.all_to_all(tile_keys, 'mem', split_axis=0, concat_axis=0, tiled=True)  7.56 us
    reshape x2, local copies, waits for them, and re-layouts, body(): memory_keys.reshape(tiles_here, rows_per_block, local_head_count, head_fe...  7.49 us
    reshape x2, local copies, waits for them, and re-layouts, body(): memory_values.reshape(tiles_here, rows_per_block, local_head_count, head_...  7.45 us
  transfers between devices with their start and end apart: 8, of which 4 were waited for; matrix products, arithmetic and copies ran while one was open for 32% of the time, Pallas kernels for 0%

commit v1 on v0

v1 whole, which is shorter than its diff:
```python
import functools
import math

import jax
import jax.numpy as jnp
from jax import lax
from jax.experimental import pallas as pl
from jax.experimental.pallas import tpu as pltpu
from jax.sharding import PartitionSpec as P


BLK = 128
DH = 128
UNITS = 5
LANES = 128
FLAG = 8
LOG2E = 1.4426950408889634
BF16 = jnp.bfloat16
F32 = jnp.float32
ANY = pl.BlockSpec(memory_space=pl.ANY)
SMEM = pl.BlockSpec(memory_space=pltpu.SMEM)
VMEM = pl.BlockSpec(memory_space=pltpu.VMEM)


def dot_nt(a, b):
    return lax.dot_general(a, b, (((1,), (1,)), ((), ())), preferred_element_type=F32)


def dot_nn(a, b):
    return lax.dot_general(a, b, (((1,), (0,)), ((), ())), preferred_element_type=F32)


def dot_tn(a, b):
    return lax.dot_general(a, b, (((0,), (0,)), ((), ())), preferred_element_type=F32)


def request_kernel(ids, request, slots, filled):
    blocks, heads, top = ids.shape
    members = request.shape[0]

    def clear(chip, carry):
        filled[chip] = 0
        for lane in range(UNITS + 1):
            request[2 * chip, 0, lane] = -1
            request[2 * chip + 1, 0, lane] = -1
        return carry

    def enter(group, over):
        block, head = group // heads, group % heads
        for t in range(top):
            tile = ids[block, head, t]
            chip = tile >> 5
            place = filled[chip]
            filled[chip] = place + 1
            code = (tile & 31) * heads + head
            request[2 * chip, 0, place] = code
            request[2 * chip + 1, 0, place] = code
            slots[group * top + t] = chip * 8 + place
            over = jnp.maximum(over, place)
        return over

    def flag(member, over):
        request[member, 0, FLAG] = (over >= UNITS).astype(jnp.int32)
        return over

    lax.fori_loop(0, members // 2, clear, 0)
    over = lax.fori_loop(0, blocks * heads, enter, jnp.int32(0))
    lax.fori_loop(0, members, flag, over)


def requests(ids, members):
    return pl.pallas_call(
        request_kernel,
        out_shape=(
            jax.ShapeDtypeStruct((members, 1, LANES), jnp.int32),
            jax.ShapeDtypeStruct((ids.size,), jnp.int32),
        ),
        in_specs=[SMEM],
        out_specs=(SMEM, SMEM),
        scratch_shapes=[pltpu.SMEM((members // 2,), jnp.int32)],
        name="requests",
    )(ids)


def gather_kernel(first, units, codes, core, keys, vals, peer_keys, peer_vals, out, stage, taken, given):
    members = codes.shape[0]

    def take(source, code, place):
        row = pl.multiple_of(((code >> 2) & 15) * BLK, BLK)
        col = pl.multiple_of((code & 3) * DH, DH)
        tile = source.at[pl.ds(row, BLK), pl.ds(col, DH)]
        return pltpu.make_async_copy(tile, stage.at[place], taken.at[place])

    def give(place):
        return pltpu.make_async_copy(stage.at[place], out.at[place], given.at[place])

    def each(step):
        def member(dest, carry):
            for unit in range(units):
                code = codes[dest, 0, first + unit]

                @pl.when(code >= 0)
                def _():
                    step(code, dest * units + unit)

            return carry

        lax.fori_loop(0, members, member, 0)

    for c, own, peer in ((0, keys, peer_keys), (1, vals, peer_vals)):

        def fetch(code, place, c=c, own=own, peer=peer):
            @pl.when((code >> 6) == c)
            def _():
                take(own, code, place).start()

            @pl.when((code >> 6) != c)
            def _():
                take(peer, code, place).start()

        @pl.when(core[0] == c)
        def _():
            each(fetch)

    def pass_on(code, place):
        take(keys, code, place).wait()
        give(place).start()

    each(pass_on)
    each(lambda code, place: give(place).wait())


def gather_tiles(codes, core, keys, vals, peer_keys, peer_vals, first, units):
    count = codes.shape[0] * units
    return pl.pallas_call(
        functools.partial(gather_kernel, first, units),
        out_shape=jax.ShapeDtypeStruct((count, BLK, DH), BF16),
        in_specs=[SMEM, SMEM, ANY, ANY, ANY, ANY],
        out_specs=ANY,
        scratch_shapes=[
            pltpu.VMEM((count, BLK, DH), BF16),
            pltpu.SemaphoreType.DMA((count,)),
            pltpu.SemaphoreType.DMA((count,)),
        ],
        name="gather_tiles",
    )(codes, core, keys, vals, peer_keys, peer_vals)


def closing_kernel(gk, gv, back, gk_out, gv_out):
    rest = gk.shape[0] - 2 * BLK
    for i, own, out in ((0, gk, gk_out), (1, gv, gv_out)):
        out[:rest] = own[:rest].astype(BF16)
        out[rest:] = (own[rest:] + back[i].astype(F32)).astype(BF16)


def closing(gk, gv, back):
    return pl.pallas_call(
        closing_kernel,
        out_shape=(jax.ShapeDtypeStruct(gk.shape, BF16), jax.ShapeDtypeStruct(gv.shape, BF16)),
        in_specs=[VMEM, VMEM, VMEM],
        out_specs=(VMEM, VMEM),
        name="closing",
    )(gk, gv, back)


def memory_kernel(units, heads, top, scale, slots, tiles, q, gm, lq, out, kbuf, vbuf, sems):
    blocks = q.shape[0] // BLK

    def copies(r):
        slot = slots[r]
        base = (slot >> 3) * 2 * units + (slot & 7)
        rows = pl.ds(pl.multiple_of((r % top) * BLK, BLK), BLK)
        return (
            pltpu.make_async_copy(tiles.at[base], kbuf.at[r // top, rows], sems.at[2 * r]),
            pltpu.make_async_copy(tiles.at[base + units], vbuf.at[r // top, rows], sems.at[2 * r + 1]),
        )

    def issue(r, carry):
        for one in copies(r):
            one.start()
        return carry

    lax.fori_loop(0, blocks * heads * top, issue, 0)
    for b in range(blocks):
        rows = slice(b * BLK, (b + 1) * BLK)
        for r in range(b * heads * top, (b + 1) * heads * top):
            for one in copies(r):
                one.wait()
        for h in range(heads):
            cols = slice(h * DH, (h + 1) * DH)
            keys = kbuf[b * heads + h]
            scores = dot_nt(q[rows, cols], keys)
            peak = jnp.max(scores, axis=-1, keepdims=True)
            expo = jnp.exp2((scores - peak) * (scale * LOG2E))
            inverse = 1.0 / jnp.sum(expo, axis=-1, keepdims=True)
            dprobs = dot_nt(gm[rows, cols], vbuf[b * heads + h])
            delta = jnp.sum(expo * dprobs, axis=-1, keepdims=True) * inverse
            dscores = (expo * (dprobs - delta)).astype(BF16)
            grad = dot_nn(dscores, keys) * (inverse * scale)
            out[rows, cols] = (grad + lq[rows, cols]).astype(BF16)


def memory_part(slots, tiles, q, gm, lq, units, heads, top, scale):
    tokens, width = q.shape
    groups = tokens // BLK * heads
    return pl.pallas_call(
        functools.partial(memory_kernel, units, heads, top, scale),
        out_shape=jax.ShapeDtypeStruct((tokens, width), BF16),
        in_specs=[SMEM, ANY, VMEM, VMEM, VMEM],
        out_specs=VMEM,
        scratch_shapes=[
            pltpu.VMEM((groups, top * BLK, DH), BF16),
            pltpu.VMEM((groups, top * BLK, DH), BF16),
            pltpu.SemaphoreType.DMA((2 * groups * top,)),
        ],
        cost_estimate=pl.CostEstimate(
            flops=6 * groups * BLK * top * BLK * DH, transcendentals=groups * BLK * top * BLK, bytes_accessed=5 << 20
        ),
        name="memory_part",
    )(slots, tiles, q, gm, lq)


def join_kernel(*refs):
    *parts, out = refs
    rows = parts[0].shape[0]
    for i, part in enumerate(parts):
        out[i * rows : (i + 1) * rows] = part[...]


def join(parts):
    rows, width = parts[0].shape
    return pl.pallas_call(
        join_kernel,
        out_shape=jax.ShapeDtypeStruct((rows * len(parts), width), parts[0].dtype),
        in_specs=[VMEM] * len(parts),
        out_specs=VMEM,
        name="join",
    )(*parts)


def head_kernel(order, go_a, go_b, w_a, w_b, out):
    part = dot_nn(
        jnp.concatenate([go_a[...], go_b[...]], axis=1), jnp.concatenate([w_a[...], w_b[...]], axis=0)
    )

    @pl.when(pl.program_id(0) == 0)
    def _():
        out[...] = part

    @pl.when(pl.program_id(0) > 0)
    def _():
        out[...] += part


def head_part(order, grad_out, w_a, w_b):
    tokens = grad_out.shape[0]
    rows, width = w_a.shape
    steps = rows // BLK
    return pl.pallas_call(
        head_kernel,
        grid_spec=pltpu.PrefetchScalarGridSpec(
            num_scalar_prefetch=1,
            grid=(steps,),
            in_specs=[
                pl.BlockSpec((tokens, BLK), lambda k, order: (0, order[0, k])),
                pl.BlockSpec((tokens, BLK), lambda k, order: (0, order[1, k])),
                pl.BlockSpec((BLK, width), lambda k, order: (k, 0)),
                pl.BlockSpec((BLK, width), lambda k, order: (k, 0)),
            ],
            out_specs=pl.BlockSpec((tokens, width), lambda k, order: (0, 0)),
        ),
        out_shape=jax.ShapeDtypeStruct((tokens, width), F32),
        cost_estimate=pl.CostEstimate(
            flops=4 * tokens * rows * width, transcendentals=0, bytes_accessed=9 << 20
        ),
        name="head_part",
    )(order, grad_out, grad_out, w_a, w_b)


def local_kernel(scale, window, start, gate, q, k, v, halo, hg, gm_out, lq_out, gk_out, gv_out, back_out):
    head = pl.program_id(0)
    share = gate[head]
    blocks = q.shape[0] // BLK
    key_blocks = [halo[0, :BLK], halo[0, BLK:]] + [k[i * BLK : (i + 1) * BLK] for i in range(blocks)]
    val_blocks = [halo[1, :BLK], halo[1, BLK:]] + [v[i * BLK : (i + 1) * BLK] for i in range(blocks)]
    key_sums = [None] * (blocks + 2)
    val_sums = [None] * (blocks + 2)
    row = lax.broadcasted_iota(jnp.int32, (BLK, 3 * BLK), 0)
    col = lax.broadcasted_iota(jnp.int32, (BLK, 3 * BLK), 1) - 2 * BLK
    for b in range(blocks):
        rows = slice(b * BLK, (b + 1) * BLK)
        grad = hg[rows, :]
        gm_out[rows, :] = (share * grad).astype(BF16)
        gl = ((1.0 - share) * grad).astype(BF16)
        qb = q[rows, :]
        keys = jnp.concatenate(key_blocks[b : b + 3], axis=0)
        vals = jnp.concatenate(val_blocks[b : b + 3], axis=0)
        allowed = (col <= row) & (col > row - window[b]) & (col + b * BLK >= -start[0])
        scores = jnp.where(allowed, dot_nt(qb, keys) * scale, -1e30)
        expo = jnp.exp(scores - jnp.max(scores, axis=-1, keepdims=True))
        probs = expo * (1.0 / jnp.sum(expo, axis=-1, keepdims=True))
        dprobs = dot_nt(gl, vals)
        delta = jnp.sum(probs * dprobs, axis=-1, keepdims=True)
        dscores = (probs * (dprobs - delta)).astype(BF16)
        probs16 = probs.astype(BF16)
        lq_out[rows, :] = dot_nn(dscores, keys) * scale
        key_grad = dot_tn(dscores, qb)
        val_grad = dot_tn(probs16, gl)
        for j in range(3):
            part = slice(j * BLK, (j + 1) * BLK)
            for sums, grads in ((key_sums, key_grad), (val_sums, val_grad)):
                sums[b + j] = grads[part] if sums[b + j] is None else sums[b + j] + grads[part]
    for i in range(2):
        back_out[0, i * BLK : (i + 1) * BLK, :] = (key_sums[i] * scale).astype(BF16)
        back_out[1, i * BLK : (i + 1) * BLK, :] = val_sums[i].astype(BF16)
    for i in range(blocks):
        gk_out[i * BLK : (i + 1) * BLK, :] = key_sums[i + 2] * scale
        gv_out[i * BLK : (i + 1) * BLK, :] = val_sums[i + 2]


def local_part(window, start, gate, q, k, v, halo, hg, scale):
    tokens, width = q.shape
    heads = width // DH
    column = pl.BlockSpec((tokens, DH), lambda h: (0, h))
    pair = pl.BlockSpec((2, 2 * BLK, DH), lambda h: (0, 0, h))
    return pl.pallas_call(
        functools.partial(local_kernel, scale),
        grid=(heads,),
        out_shape=(
            jax.ShapeDtypeStruct((tokens, width), BF16),
            jax.ShapeDtypeStruct((tokens, width), F32),
            jax.ShapeDtypeStruct((tokens, width), F32),
            jax.ShapeDtypeStruct((tokens, width), F32),
            jax.ShapeDtypeStruct((2, 2 * BLK, width), BF16),
        ),
        in_specs=[SMEM, SMEM, SMEM, column, column, column, pair, column],
        out_specs=(column, column, column, column, pair),
        cost_estimate=pl.CostEstimate(
            flops=10 * tokens * 3 * BLK * width, transcendentals=tokens * 3 * BLK * heads, bytes_accessed=6 << 20
        ),
        name="local_part",
    )(window, start, gate, q, k, v, halo, hg)


def place_of(x, y, core):
    return (x % 4) * 8 + (y % 4) * 2 + core


def torus(shift, phase):
    pairs = []
    for x in range(4):
        for y in range(4):
            for core in range(2):
                dx, dy = (shift, 0) if core == phase else (0, shift)
                pairs.append((place_of(x, y, core), place_of(x + dx, y + dy, core)))
    return pairs


def arrival(me):
    x, y, core = me >> 3, (me >> 1) & 3, me & 1
    step = jnp.arange(16, dtype=jnp.int32)
    first, second = step & 3, step >> 2
    south = place_of(x - first, y - second, 0)
    north = place_of(x - second, y - first, 1)
    return jnp.where(core == 0, jnp.stack([south, north]), jnp.stack([north, south]))


def body(
    queries,
    local_keys,
    local_values,
    memory_keys,
    memory_values,
    grad_out,
    out_weight,
    gate_logits,
    tile_ids,
    window,
):
    _, heads, top = tile_ids.shape
    members = lax.axis_size("mem")
    me = lax.axis_index("mem")
    core = (me & 1).reshape(1)
    scale = 1.0 / math.sqrt(DH)
    tokens = queries.shape[0]

    request, slots = requests(tile_ids, members)
    codes = lax.all_to_all(request, "mem", split_axis=0, concat_axis=0, tiled=True)

    partner = [(i, i ^ 1) for i in range(members)]
    peer_keys = lax.ppermute(memory_keys, "mem", partner)
    peer_vals = lax.ppermute(memory_values, "mem", partner)
    rows = [out_weight] + [lax.ppermute(out_weight, "mem", torus(shift, 0)) for shift in (1, 2, 3)]
    sources = (codes, core, memory_keys, memory_values, peer_keys, peer_vals)
    sent = gather_tiles(*sources, 0, UNITS).reshape(members, UNITS, BLK, DH)
    band = join(rows)
    bands = [band] + [lax.ppermute(band, "mem", torus(shift, 1)) for shift in (1, 2, 3)]
    halo = jnp.stack([local_keys[tokens - 2 * BLK :], local_values[tokens - 2 * BLK :]])
    halo = lax.ppermute(halo, "mem", [(i, i + 1) for i in range(members - 1)])
    tiles = lax.all_to_all(sent, "mem", split_axis=0, concat_axis=0, tiled=True)

    w_own = join(bands)
    w_peer = lax.ppermute(w_own, "mem", partner)
    head_grad = head_part(arrival(me), grad_out, w_own, w_peer)
    gate = jax.nn.sigmoid(gate_logits)
    start = (me * tokens).reshape(1)
    gm, lq, gk, gv, back = local_part(
        window, start, gate, queries, local_keys, local_values, halo, head_grad, scale
    )
    back = lax.ppermute(back, "mem", [(i + 1, i) for i in range(members - 1)])
    grad_keys, grad_values = closing(gk, gv, back)

    def usual():
        flat = tiles.reshape(members * UNITS, BLK, DH)
        return memory_part(slots, flat, queries, gm, lq, UNITS, heads, top, scale)

    def with_sixth():
        sixth = gather_tiles(*sources, UNITS, 1).reshape(members, 1, BLK, DH)
        sixth = lax.all_to_all(sixth, "mem", split_axis=0, concat_axis=0, tiled=True)
        flat = jnp.concatenate([tiles, sixth], axis=1).reshape(members * (UNITS + 1), BLK, DH)
        return memory_part(slots, flat, queries, gm, lq, UNITS + 1, heads, top, scale)

    grad_queries = lax.cond(jnp.max(codes[:, 0, FLAG]) > 0, with_sixth, usual)
    return grad_queries, grad_keys, grad_values


def solution(mesh):
    in_specs = (
        P("mem", "mp"),
        P("mem", "mp"),
        P("mem", "mp"),
        P("mem", "mp"),
        P("mem", "mp"),
        P("mem", None),
        P("mem", "mp"),
        P("mp"),
        P("mem", "mp", None),
        P("mem"),
    )
    out_specs = (P("mem", "mp"), P("mem", "mp"), P("mem", "mp"))

    return jax.shard_map(body, mesh=mesh, in_specs=in_specs, out_specs=out_specs, check_vma=False)
```

time: 180 us -> 179 us (level)
  Pallas kernels: 0 us -> 48 us
  local copies, waits for them, and re-layouts: 47.1 us -> 2.19 us
  waiting for transfers between devices: 58.3 us -> 88.2 us
  matrix products: 16.2 us -> 0 us
  between operations: 14.6 us -> 1.6 us
  other arithmetic: 10.4 us -> 1.9 us
  starting transfers between devices: 32.2 us -> 36.1 us
    ppermute x4 -> x11, waiting for transfers between devices: 6.21 us -> 81.3 us  [the longest x3 59 us: body(): lax.ppermute(out_weight, 'mem', torus(shift, 0))]
    all_to_all x2 -> x1, waiting for transfers between devices: 51.4 us -> 0.01 us  [body(): tiles = lax.all_to_all(sent, 'mem', split_axis=0, concat_axis=0, tiled=True)]
    pallas_call x0 -> x8, Pallas kernels: none -> 48 us  [the longest x1 13.5 us: head_part(): pl.pallas_call(head_kernel, grid_spec=pltpu.PrefetchScalarGridSpec(num_sc...]
    reshape x11 -> x0, local copies, waits for them, and re-layouts: 20.1 us -> none  [the longest x2 7.49 us: body(): memory_keys.reshape(tiles_here, rows_per_block, local_head_count, head_fe...]
    gather x4 -> x0, local copies, waits for them, and re-layouts: 17.5 us -> none  [the longest x2 7.98 us: regroup(): array.reshape((tile_holders * memory_slots,) + array.shape[2:])]
    ppermute x4 -> x11, starting transfers between devices: 10.5 us -> 24.2 us  [the longest x1 7.59 us: body(): w_peer = lax.ppermute(w_own, 'mem', partner)]
    dot_general x18 -> x0, matrix products: 11.3 us -> none  [the longest x1 4.87 us: body(): jnp.dot(grad_out, lax.all_gather(out_weight, 'mem', axis=0, tiled=True),...]
    all_to_all x2 -> x1, starting transfers between devices: 13.1 us -> 6.17 us  [body(): tiles = lax.all_to_all(sent, 'mem', split_axis=0, concat_axis=0, tiled=True)]
  transfers between devices with their start and end apart: 8 -> 13, of which waited for: 4 -> 6; matrix products, arithmetic and copies ran while one was open for 32% -> 1% of each run, Pallas kernels for 0% -> 18%
where the time goes in v1:
time: 179 us; the launch traced here: 178 us
  waiting for transfers between devices  88.2 us (49%)
  Pallas kernels  48 us (27%)
  starting transfers between devices  36.1 us (20%)
  local copies, waits for them, and re-layouts  2.19 us (1%)
  other arithmetic  1.9 us (1%)
    ppermute x3, waiting for transfers between devices, body(): lax.ppermute(out_weight, 'mem', torus(shift, 0))  59 us
    ppermute x3, waiting for transfers between devices, body(): lax.ppermute(band, 'mem', torus(shift, 1))  14.8 us
    pallas_call x1, Pallas kernels, head_part(): pl.pallas_call(head_kernel, grid_spec=pltpu.PrefetchScalarGridSpec(num_sc...  13.5 us
    pallas_call x1, Pallas kernels, local_part(): pl.pallas_call(functools.partial(local_kernel, scale), grid=(heads,), out...  8.99 us
    pallas_call x1, Pallas kernels, memory_part(): pl.pallas_call(functools.partial(memory_kernel, units, heads, top, scale)...  8.62 us
    ppermute x1, starting transfers between devices, body(): w_peer = lax.ppermute(w_own, 'mem', partner)  7.59 us
    ppermute x1, waiting for transfers between devices, body(): back = lax.ppermute(back, 'mem', [(i + 1, i) for i in range(members - 1)])  7.5 us
    pallas_call x1, Pallas kernels, gather_tiles(): pl.pallas_call(functools.partial(gather_kernel, first, units), out_shape=...  7 us
  transfers between devices with their start and end apart: 13, of which 6 were waited for; matrix products, arithmetic and copies ran while one was open for 1% of the time, Pallas kernels for 18%

profile of v1, /device:TPU:1, one launch (start us, length us, event | category | flops | bytes accessed | tf_op | source)
XLA Modules:
  0.0 178.2 jit_solution(17465633779983023293)
XLA Ops:
  0.6 3.3 %collective-permute-start = (bf16[2048,512]{1,0:T(8,128)(2,1)}, bf16[2048,512]{1,0:T(8,128)(2,1)S(1)}, u32[]{:S(2)}, u32[]{:S(2)}) collective-permute-start(bf16[2048,512]{1,0:T(8,128)(2,1)} %keys.1), channel_id=1, source_target_pairs={{0,8},{8,0},{16,24},{24,16},{32,40},{40,32},{48,56},{56,48},{64,72... | collective-permute-start | bytes 6291464 | tf_op jit(solution)/shard_map/ppermute | solution.py:391
  3.9 0.1 collective-permute-start.1
  4.0 2.6 %requests.1 = (s32[32,1,128]{2,1,0:T(1,128)}, s32[48]{0:T(128)S(1)}) custom-call(s32[3,4,4]{2,1,0:T(4,128)} %ids.1), custom_call_target="tpu_custom_call" | custom-call | tf_op jit(solution)/shard_map/requests/pallas_call | solution.py:72
  6.6 5.8 %all-to-all-start.1 = ((s32[32,1,128]{2,1,0:T(1,128)}), s32[32,1,128]{2,1,0:T(1,128)S(1)}, u32[]{:S(2)}, u32[]{:S(2)}) async-start(s32[32,1,128]{2,1,0:T(1,128)} %get-tuple-element.63), calls=%async_computation.1 | async-start | bytes 32768 | tf_op jit(solution)/shard_map/all_to_all | solution.py:388
  12.4 6.9 %all-to-all-done.1.codes = s32[32,1,128]{2,1,0:T(1,128)S(1)} async-done(((s32[32,1,128]{2,1,0:T(1,128)}), s32[32,1,128]{2,1,0:T(1,128)S(1)}, u32[]{:S(2)}, u32[]{:S(2)}) %all-to-all-start.1) | async-done | bytes 16416 | tf_op jit(solution)/shard_map/all_to_all | solution.py:388
  19.3 0.0 collective-permute-done.peer_keys
  19.3 0.0 collective-permute-done.1.peer_vals
  19.3 7.0 %gather_tiles.3 = bf16[160,128,128]{2,1,0:T(8,128)(2,1)} custom-call(s32[32,1,128]{2,1,0:T(1,128)S(1)} %all-to-all-done.1.codes, s32[1]{0:T(128)} %bitcast.5.core, bf16[2048,512]{1,0:T(8,128)(2,1)} %keys.1, bf16[2048,512]{1,0:T(8,128)(2,1)} %vals.1, bf16[2048,512]{1,0:T(8,128)(2,1)S(1)} %collective-permute-done.peer_keys, ...), custom_call_target="tpu_custom_call" | custom-call | tf_op jit(solution)/shard_map/gather_tiles/pallas_call | solution.py:135
  26.3 0.0 copy-start.9
  26.3 6.2 %all-to-all-start.2 = ((bf16[32,5,128,128]{3,2,1,0:T(8,128)(2,1)}), bf16[32,5,128,128]{3,2,1,0:T(8,128)(2,1)}, u32[]{:S(2)}, u32[]{:S(2)}) async-start(bf16[32,5,128,128]{3,2,1,0:T(8,128)(2,1)} %bitcast.13), calls=%async_computation.2 | async-start | bytes 10485760 | tf_op jit(solution)/shard_map/all_to_all | solution.py:400
  32.5 0.0 copy-start.7
  32.5 0.0 copy-start.8
  32.5 0.0 copy-start.13
  32.5 3.0 %collective-permute-start.4 = (bf16[128,512]{1,0:T(8,128)(2,1)S(1)}, bf16[128,512]{1,0:T(8,128)(2,1)S(1)}, u32[]{:S(2)}, u32[]{:S(2)}) collective-permute-start(bf16[128,512]{1,0:T(8,128)(2,1)S(1)} %copy-done.9), channel_id=1, source_target_pairs={{0,128},{8,40},{16,144},{24,56},{32,160},{40,8},{48,176},{56,24},{... | collective-permute-start | bytes 393224 | tf_op jit(solution)/shard_map/ppermute | solution.py:393
  35.5 0.3 collective-permute-start.3
  35.8 2.4 %collective-permute-start.5 = (bf16[128,512]{1,0:T(8,128)(2,1)S(1)}, bf16[128,512]{1,0:T(8,128)(2,1)S(1)}, u32[]{:S(2)}, u32[]{:S(2)}) collective-permute-start(bf16[128,512]{1,0:T(8,128)(2,1)S(1)} %copy-done.9), channel_id=1, source_target_pairs={{0,192},{8,56},{16,208},{24,8},{32,224},{40,24},{48,240},{56,40},{... | collective-permute-start | bytes 393224 | tf_op jit(solution)/shard_map/ppermute | solution.py:393
  38.2 57.6 %collective-permute-done.4.refs_2_ = bf16[128,512]{1,0:T(8,128)(2,1)S(1)} collective-permute-done((bf16[128,512]{1,0:T(8,128)(2,1)S(1)}, bf16[128,512]{1,0:T(8,128)(2,1)S(1)}, u32[]{:S(2)}, u32[]{:S(2)}) %collective-permute-start.4) | collective-permute-done | bytes 131104 | tf_op jit(solution)/shard_map/ppermute | solution.py:393
  95.8 1.4 collective-permute-done.3.refs_1_
  97.2 0.0 collective-permute-done.5.refs_3_
  97.2 0.0 copy-done.10
  97.2 0.6 copy-done.11
  97.9 0.7 copy-done.12
  98.5 1.9 %join.2.refs_0_ = bf16[512,512]{1,0:T(8,128)(2,1)} custom-call(bf16[128,512]{1,0:T(8,128)(2,1)} %refs_0_.1, bf16[128,512]{1,0:T(8,128)(2,1)} %copy-done.11, bf16[128,512]{1,0:T(8,128)(2,1)} %copy-done.10, bf16[128,512]{1,0:T(8,128)(2,1)} %copy-done.12), custom_call_target="tpu_custom_call" | custom-call | tf_op jit(solution)/shard_map/join/pallas_call | solution.py:232
  100.4 1.5 collective-permute-start.8
  101.9 0.0 collective-permute-start.7
  101.9 0.6 collective-permute-start.6
  102.5 11.5 %collective-permute-done.8.refs_3_ = bf16[512,512]{1,0:T(8,128)(2,1)S(1)} collective-permute-done((bf16[512,512]{1,0:T(8,128)(2,1)}, bf16[512,512]{1,0:T(8,128)(2,1)S(1)}, u32[]{:S(2)}, u32[]{:S(2)}) %collective-permute-start.8) | collective-permute-done | bytes 524320 | tf_op jit(solution)/shard_map/ppermute | solution.py:397
  114.0 0.0 collective-permute-done.7.refs_2_
  114.0 3.3 %collective-permute-done.6.refs_1_ = bf16[512,512]{1,0:T(8,128)(2,1)S(1)} collective-permute-done((bf16[512,512]{1,0:T(8,128)(2,1)}, bf16[512,512]{1,0:T(8,128)(2,1)S(1)}, u32[]{:S(2)}, u32[]{:S(2)}) %collective-permute-start.6) | collective-permute-done | bytes 524320 | tf_op jit(solution)/shard_map/ppermute | solution.py:397
  117.3 0.8 copy-done.6
  118.1 3.0 %join.3.w_a = bf16[2048,512]{1,0:T(8,128)(2,1)} custom-call(bf16[512,512]{1,0:T(8,128)(2,1)} %join.2.refs_0_, bf16[512,512]{1,0:T(8,128)(2,1)} %copy-done.6, bf16[512,512]{1,0:T(8,128)(2,1)} %copy-done.5, bf16[512,512]{1,0:T(8,128)(2,1)} %copy-done.4), custom_call_target="tpu_custom_call" | custom-call | tf_op jit(solution)/shard_map/join/pallas_call | solution.py:232
  121.1 7.6 %collective-permute-start.9 = (bf16[2048,512]{1,0:T(8,128)(2,1)}, bf16[2048,512]{1,0:T(8,128)(2,1)}, u32[]{:S(2)}, u32[]{:S(2)}) collective-permute-start(bf16[2048,512]{1,0:T(8,128)(2,1)} %join.3.w_a), channel_id=1, source_target_pairs={{0,8},{8,0},{16,24},{24,16},{32,40},{40,32},{48,56},{56,48},{64,72... | collective-permute-start | bytes 6291464 | tf_op jit(solution)/shard_map/ppermute | solution.py:403
  128.7 0.0 copy-done.7
  128.7 0.1 pad_maximum_fusion.1
  128.8 3.6 %collective-permute-start.2 = (bf16[2,256,512]{2,1,0:T(8,128)(2,1)S(1)}, bf16[2,256,512]{2,1,0:T(8,128)(2,1)}, u32[]{:S(2)}, u32[]{:S(2)}) collective-permute-start(bf16[2,256,512]{2,1,0:T(8,128)(2,1)S(1)} %pad_maximum_fusion.1), channel_id=1, source_target_pairs={{0,8},{8,16},{16,24},{24,32},{32,40},{40,48},{48,56},{56,64},{64,7... | collective-permute-start | bytes 1572872 | tf_op jit(solution)/shard_map/ppermute | solution.py:399
  132.4 0.6 add_select_fusion.order
  133.0 0.5 add_divide_fusion.gate
  133.5 0.0 collective-permute-done.9.w_b
  133.5 13.5 %head_part.1.hg = f32[384,512]{1,0:T(8,128)} custom-call(s32[2,16]{1,0:T(2,128)} %add_select_fusion.order, bf16[384,4096]{1,0:T(8,128)(2,1)} %go_b.1, bf16[384,4096]{1,0:T(8,128)(2,1)} %go_b.1, bf16[2048,512]{1,0:T(8,128)(2,1)} %join.3.w_a, bf16[2048,512]{1,0:T(8,128)(2,1)} %collective-permute-done.9.w_b), custom_call_target="tpu_custom_call" | custom-call | flops 1610612736 | bytes 9437184 | tf_op jit(solution)/shard_map/head_part/pallas_call | solution.py:259
  147.0 0.0 collective-permute-done.2.halo
  147.0 9.0 %local_part.1 = (bf16[384,512]{1,0:T(8,128)(2,1)}, f32[384,512]{1,0:T(8,128)S(1)}, f32[384,512]{1,0:T(8,128)}, f32[384,512]{1,0:T(8,128)}, bf16[2,256,512]{2,1,0:T(8,128)(2,1)}) custom-call(s32[3]{0:T(128)} %window.1, s32[1]{0:T(128)} %bitcast.7.start, f32[4]{0:T(128)} %add_divide_fusion.gate, bf16[384,512]{1,0:T(8,128)(2,1)S(1)} %copy-done.2, ...), custom_call_target="tpu_custom_call" | custom-call | flops 754974720 | bytes 6291456 | tf_op jit(solution)/shard_map/local_part/pallas_call | solution.py:326
  156.0 1.9 %collective-permute-start.10 = (bf16[2,256,512]{2,1,0:T(8,128)(2,1)}, bf16[2,256,512]{2,1,0:T(8,128)(2,1)}, u32[]{:S(2)}, u32[]{:S(2)}) collective-permute-start(bf16[2,256,512]{2,1,0:T(8,128)(2,1)} %get-tuple-element.69), channel_id=1, source_target_pairs={{8,0},{16,8},{24,16},{32,24},{40,32},{48,40},{56,48},{64,56},{72,6... | collective-permute-start | bytes 1572872 | tf_op jit(solution)/shard_map/ppermute | solution.py:410
  157.9 0.7 slice_reduce_fusion
  159.3 7.5 %collective-permute-done.10.back = bf16[2,256,512]{2,1,0:T(8,128)(2,1)} collective-permute-done((bf16[2,256,512]{2,1,0:T(8,128)(2,1)}, bf16[2,256,512]{2,1,0:T(8,128)(2,1)}, u32[]{:S(2)}, u32[]{:S(2)}) %collective-permute-start.10) | collective-permute-done | bytes 524320 | tf_op jit(solution)/shard_map/ppermute | solution.py:410
  166.8 2.5 %closing.1 = (bf16[384,512]{1,0:T(8,128)(2,1)}, bf16[384,512]{1,0:T(8,128)(2,1)}) custom-call(f32[384,512]{1,0:T(8,128)} %get-tuple-element.67.gk, f32[384,512]{1,0:T(8,128)} %get-tuple-element.68.gv, bf16[2,256,512]{2,1,0:T(8,128)(2,1)} %collective-permute-done.10.back), custom_call_target="tpu_custom_call" | custom-call | tf_op jit(solution)/shard_map/closing/pallas_call | solution.py:157
  169.3 0.0 all-to-all-done.2
  169.3 8.8 %conditional.1 = (bf16[384,512]{1,0:T(8,128)(2,1)}) conditional(s32[]{:T(128)} %convert_element_type.3, (bf16[32,5,128,128]{3,2,1,0:T(8,128)(2,1)}, s32[48]{0:T(128)S(1)}, bf16[384,512]{1,0:T(8,128)(2,1)S(1)}, bf16[384,512]{1,0:T(8,128)(2,1)}, f32[384,512]{1,0:T(8,128)S(1)}) %tuple.23, (s32[32,1,128]{2,1,0:T(1,128)S(1)}, s32[1]{0:T(128)}, ...), branch_computations={%region_1.2_spmd, %region_2.3_spmd} | conditional | flops 607125504 | bytes 21495844 | solution.py:423
  169.4 8.6 %memory_part.2 = bf16[384,512]{1,0:T(8,128)(2,1)} custom-call(s32[48]{0:T(128)S(1)} %get-tuple-element.20.slots, bf16[160,128,128]{2,1,0:T(8,128)(2,1)} %bitcast.tiles, bf16[384,512]{1,0:T(8,128)(2,1)S(1)} %get-tuple-element.37.q, bf16[384,512]{1,0:T(8,128)(2,1)} %get-tuple-element.38.gm, f32[384,512]{1,0:T(8,128)S(1)} %get-tuple-element.39.lq), custom_call_target="tpu_custom_call" | custom-call | flops 603979776 | bytes 5242880 | tf_op jit(solution)/shard_map/cond/branch_0_fun/memory_part/pallas_call | solution.py:206
  (19 shorter events, 0.1 us)
Async XLA Ops:
  0.6 18.7 %collective-permute-start = (bf16[2048,512]{1,0:T(8,128)(2,1)}, bf16[2048,512]{1,0:T(8,128)(2,1)S(1)}, u32[]{:S(2)}, u32[]{:S(2)}) collective-permute-start(bf16[2048,512]{1,0:T(8,128)(2,1)} %keys.1), channel_id=1, source_target_pairs={{0,8},{8,0},{16,24},{24,16},{32,40},{40,32},{48,56},{56,48},{64,72... | collective-permute-start | bytes 6291464 | tf_op jit(solution)/shard_map/ppermute | solution.py:391
  3.9 15.4 %collective-permute-start.1 = (bf16[2048,512]{1,0:T(8,128)(2,1)}, bf16[2048,512]{1,0:T(8,128)(2,1)}, u32[]{:S(2)}, u32[]{:S(2)}) collective-permute-start(bf16[2048,512]{1,0:T(8,128)(2,1)} %vals.1), channel_id=1, source_target_pairs={{0,8},{8,0},{16,24},{24,16},{32,40},{40,32},{48,56},{56,48},{64,72... | collective-permute-start | bytes 6291464 | tf_op jit(solution)/shard_map/ppermute | solution.py:392
  6.6 12.7 %all-to-all-start.1 = ((s32[32,1,128]{2,1,0:T(1,128)}), s32[32,1,128]{2,1,0:T(1,128)S(1)}, u32[]{:S(2)}, u32[]{:S(2)}) async-start(s32[32,1,128]{2,1,0:T(1,128)} %get-tuple-element.63), calls=%async_computation.1 | async-start | bytes 32768 | tf_op jit(solution)/shard_map/all_to_all | solution.py:388
  19.3 7.0 %copy-start.1 = (bf16[2048,512]{1,0:T(8,128)(2,1)}, bf16[2048,512]{1,0:T(8,128)(2,1)S(1)}, u32[]{:S(2)}) copy-start(bf16[2048,512]{1,0:T(8,128)(2,1)S(1)} %collective-permute-done.peer_keys) | copy-start | bytes 6291460
  26.3 6.2 %copy-start.9 = (bf16[128,512]{1,0:T(8,128)(2,1)S(1)}, bf16[128,512]{1,0:T(8,128)(2,1)}, u32[]{:S(2)}) copy-start(bf16[128,512]{1,0:T(8,128)(2,1)} %refs_0_.1) | copy-start | bytes 393220
  26.3 143.0 %all-to-all-start.2 = ((bf16[32,5,128,128]{3,2,1,0:T(8,128)(2,1)}), bf16[32,5,128,128]{3,2,1,0:T(8,128)(2,1)}, u32[]{:S(2)}, u32[]{:S(2)}) async-start(bf16[32,5,128,128]{3,2,1,0:T(8,128)(2,1)} %bitcast.13), calls=%async_computation.2 | async-start | bytes 10485760 | tf_op jit(solution)/shard_map/all_to_all | solution.py:400
  32.5 96.2 %copy-start.7 = (bf16[384,512]{1,0:T(8,128)(2,1)S(1)}, bf16[384,512]{1,0:T(8,128)(2,1)}, u32[]{:S(2)}) copy-start(bf16[384,512]{1,0:T(8,128)(2,1)} %k.1) | copy-start | bytes 1179652
  32.5 96.2 %copy-start.8 = (bf16[384,512]{1,0:T(8,128)(2,1)S(1)}, bf16[384,512]{1,0:T(8,128)(2,1)}, u32[]{:S(2)}) copy-start(bf16[384,512]{1,0:T(8,128)(2,1)} %v.1) | copy-start | bytes 1179652
  32.5 100.4 %copy-start.13 = (f32[4]{0:T(128)S(1)}, f32[4]{0:T(128)}, u32[]{:S(2)}) copy-start(f32[4]{0:T(128)} %param.19) | copy-start | bytes 52
  32.5 63.2 %collective-permute-start.4 = (bf16[128,512]{1,0:T(8,128)(2,1)S(1)}, bf16[128,512]{1,0:T(8,128)(2,1)S(1)}, u32[]{:S(2)}, u32[]{:S(2)}) collective-permute-start(bf16[128,512]{1,0:T(8,128)(2,1)S(1)} %copy-done.9), channel_id=1, source_target_pairs={{0,128},{8,40},{16,144},{24,56},{32,160},{40,8},{48,176},{56,24},{... | collective-permute-start | bytes 393224 | tf_op jit(solution)/shard_map/ppermute | solution.py:393
  35.5 61.7 %collective-permute-start.3 = (bf16[128,512]{1,0:T(8,128)(2,1)S(1)}, bf16[128,512]{1,0:T(8,128)(2,1)S(1)}, u32[]{:S(2)}, u32[]{:S(2)}) collective-permute-start(bf16[128,512]{1,0:T(8,128)(2,1)S(1)} %copy-done.9), channel_id=1, source_target_pairs={{0,64},{8,24},{16,80},{24,40},{32,96},{40,56},{48,112},{56,8},{64,... | collective-permute-start | bytes 393224 | tf_op jit(solution)/shard_map/ppermute | solution.py:393
  35.8 61.4 %collective-permute-start.5 = (bf16[128,512]{1,0:T(8,128)(2,1)S(1)}, bf16[128,512]{1,0:T(8,128)(2,1)S(1)}, u32[]{:S(2)}, u32[]{:S(2)}) collective-permute-start(bf16[128,512]{1,0:T(8,128)(2,1)S(1)} %copy-done.9), channel_id=1, source_target_pairs={{0,192},{8,56},{16,208},{24,8},{32,224},{40,24},{48,240},{56,40},{... | collective-permute-start | bytes 393224 | tf_op jit(solution)/shard_map/ppermute | solution.py:393
  95.8 1.4 copy-start.10
  97.2 0.7 copy-start.11
  97.9 0.7 copy-start.12
  100.4 13.6 %collective-permute-start.8 = (bf16[512,512]{1,0:T(8,128)(2,1)}, bf16[512,512]{1,0:T(8,128)(2,1)S(1)}, u32[]{:S(2)}, u32[]{:S(2)}) collective-permute-start(bf16[512,512]{1,0:T(8,128)(2,1)} %join.2.refs_0_), channel_id=1, source_target_pairs={{0,48},{8,200},{16,0},{24,216},{32,16},{40,232},{48,32},{56,248},{... | collective-permute-start | bytes 1572872 | tf_op jit(solution)/shard_map/ppermute | solution.py:397
  101.9 12.1 %collective-permute-start.7 = (bf16[512,512]{1,0:T(8,128)(2,1)}, bf16[512,512]{1,0:T(8,128)(2,1)S(1)}, u32[]{:S(2)}, u32[]{:S(2)}) collective-permute-start(bf16[512,512]{1,0:T(8,128)(2,1)} %join.2.refs_0_), channel_id=1, source_target_pairs={{0,32},{8,136},{16,48},{24,152},{32,0},{40,168},{48,16},{56,184},{... | collective-permute-start | bytes 1572872 | tf_op jit(solution)/shard_map/ppermute | solution.py:397
  101.9 15.4 %collective-permute-start.6 = (bf16[512,512]{1,0:T(8,128)(2,1)}, bf16[512,512]{1,0:T(8,128)(2,1)S(1)}, u32[]{:S(2)}, u32[]{:S(2)}) collective-permute-start(bf16[512,512]{1,0:T(8,128)(2,1)} %join.2.refs_0_), channel_id=1, source_target_pairs={{0,16},{8,72},{16,32},{24,88},{32,48},{40,104},{48,0},{56,120},{64... | collective-permute-start | bytes 1572872 | tf_op jit(solution)/shard_map/ppermute | solution.py:397
  114.0 3.3 %copy-start.4 = (bf16[512,512]{1,0:T(8,128)(2,1)}, bf16[512,512]{1,0:T(8,128)(2,1)S(1)}, u32[]{:S(2)}) copy-start(bf16[512,512]{1,0:T(8,128)(2,1)S(1)} %collective-permute-done.8.refs_3_) | copy-start | bytes 1572868
  114.0 3.3 %copy-start.5 = (bf16[512,512]{1,0:T(8,128)(2,1)}, bf16[512,512]{1,0:T(8,128)(2,1)S(1)}, u32[]{:S(2)}) copy-start(bf16[512,512]{1,0:T(8,128)(2,1)S(1)} %collective-permute-done.7.refs_2_) | copy-start | bytes 1572868
  117.3 0.8 copy-start.6
  121.1 12.4 %collective-permute-start.9 = (bf16[2048,512]{1,0:T(8,128)(2,1)}, bf16[2048,512]{1,0:T(8,128)(2,1)}, u32[]{:S(2)}, u32[]{:S(2)}) collective-permute-start(bf16[2048,512]{1,0:T(8,128)(2,1)} %join.3.w_a), channel_id=1, source_target_pairs={{0,8},{8,0},{16,24},{24,16},{32,40},{40,32},{48,56},{56,48},{64,72... | collective-permute-start | bytes 6291464 | tf_op jit(solution)/shard_map/ppermute | solution.py:403
  128.8 18.2 %collective-permute-start.2 = (bf16[2,256,512]{2,1,0:T(8,128)(2,1)S(1)}, bf16[2,256,512]{2,1,0:T(8,128)(2,1)}, u32[]{:S(2)}, u32[]{:S(2)}) collective-permute-start(bf16[2,256,512]{2,1,0:T(8,128)(2,1)S(1)} %pad_maximum_fusion.1), channel_id=1, source_target_pairs={{0,8},{8,16},{16,24},{24,32},{32,40},{40,48},{48,56},{56,64},{64,7... | collective-permute-start | bytes 1572872 | tf_op jit(solution)/shard_map/ppermute | solution.py:399
  133.5 13.5 %copy-start.2 = (bf16[384,512]{1,0:T(8,128)(2,1)S(1)}, bf16[384,512]{1,0:T(8,128)(2,1)}, u32[]{:S(2)}) copy-start(bf16[384,512]{1,0:T(8,128)(2,1)} %q.1) | copy-start | bytes 1179652
  133.5 35.8 %copy-start = (bf16[2048,512]{1,0:T(8,128)(2,1)S(1)}, bf16[2048,512]{1,0:T(8,128)(2,1)}, u32[]{:S(2)}) copy-start(bf16[2048,512]{1,0:T(8,128)(2,1)} %keys.1) | copy-start | bytes 6291460
  156.0 10.8 %collective-permute-start.10 = (bf16[2,256,512]{2,1,0:T(8,128)(2,1)}, bf16[2,256,512]{2,1,0:T(8,128)(2,1)}, u32[]{:S(2)}, u32[]{:S(2)}) collective-permute-start(bf16[2,256,512]{2,1,0:T(8,128)(2,1)} %get-tuple-element.69), channel_id=1, source_target_pairs={{8,0},{16,8},{24,16},{32,24},{40,32},{48,40},{56,48},{64,56},{72,6... | collective-permute-start | bytes 1572872 | tf_op jit(solution)/shard_map/ppermute | solution.py:410

commit v2 on v1

--- a/solution.py
+++ b/solution.py
@@ -18,6 +18,7 @@
 BF16 = jnp.bfloat16
 F32 = jnp.float32
 ANY = pl.BlockSpec(memory_space=pl.ANY)
+HBM = pl.BlockSpec(memory_space=pltpu.HBM)
 SMEM = pl.BlockSpec(memory_space=pltpu.SMEM)
 VMEM = pl.BlockSpec(memory_space=pltpu.VMEM)
 
@@ -34,12 +35,14 @@
     return lax.dot_general(a, b, (((0,), (0,)), ((), ())), preferred_element_type=F32)
 
 
-def request_kernel(ids, request, slots, filled):
+def request_kernel(ids, request, slots, filled, third):
     blocks, heads, top = ids.shape
     members = request.shape[0]
 
     def clear(chip, carry):
-        filled[chip] = 0
+        filled[2 * chip] = 0
+        filled[2 * chip + 1] = 0
+        third[chip] = 2
         for lane in range(UNITS + 1):
             request[2 * chip, 0, lane] = -1
             request[2 * chip + 1, 0, lane] = -1
@@ -49,9 +52,12 @@
         block, head = group // heads, group % heads
         for t in range(top):
             tile = ids[block, head, t]
-            chip = tile >> 5
-            place = filled[chip]
-            filled[chip] = place + 1
+            owner, chip = tile >> 4, tile >> 5
+            have = filled[owner]
+            filled[owner] = have + 1
+            spare = third[chip]
+            third[chip] = jnp.where(have == 2, UNITS, spare)
+            place = jnp.where(have == 2, spare, jnp.where((owner & 1) == 0, have, UNITS - 1 - have))
             code = (tile & 31) * heads + head
             request[2 * chip, 0, place] = code
             request[2 * chip + 1, 0, place] = code
@@ -77,7 +83,7 @@
         ),
         in_specs=[SMEM],
         out_specs=(SMEM, SMEM),
-        scratch_shapes=[pltpu.SMEM((members // 2,), jnp.int32)],
+        scratch_shapes=[pltpu.SMEM((members,), jnp.int32), pltpu.SMEM((members // 2,), jnp.int32)],
         name="requests",
     )(ids)
 
@@ -85,62 +91,67 @@
 def gather_kernel(first, units, codes, core, keys, vals, peer_keys, peer_vals, out, stage, taken, given):
     members = codes.shape[0]
 
-    def take(source, code, place):
-        row = pl.multiple_of(((code >> 2) & 15) * BLK, BLK)
-        col = pl.multiple_of((code & 3) * DH, DH)
-        tile = source.at[pl.ds(row, BLK), pl.ds(col, DH)]
-        return pltpu.make_async_copy(tile, stage.at[place], taken.at[place])
-
-    def give(place):
-        return pltpu.make_async_copy(stage.at[place], out.at[place], given.at[place])
-
-    def each(step):
+    def fetch_all(sources):
         def member(dest, carry):
             for unit in range(units):
                 code = codes[dest, 0, first + unit]
-
-                @pl.when(code >= 0)
-                def _():
-                    step(code, dest * units + unit)
-
+                row = pl.multiple_of(((code >> 2) & 15) * BLK, BLK)
+                col = pl.multiple_of((code & 3) * DH, DH)
+
+                def fetch(source):
+                    tile = source.at[pl.ds(row, BLK), pl.ds(col, DH)]
+                    pltpu.make_async_copy(tile, stage.at[dest, unit], taken.at[dest, unit]).start()
+
+                if first + unit in (2, UNITS):
+                    for side in range(2):
+                        pl.when((code >> 6) == side)(functools.partial(fetch, sources[side]))
+                else:
+                    pl.when(code >= 0)(functools.partial(fetch, sources[(first + unit) // 3]))
             return carry
 
         lax.fori_loop(0, members, member, 0)
 
-    for c, own, peer in ((0, keys, peer_keys), (1, vals, peer_vals)):
-
-        def fetch(code, place, c=c, own=own, peer=peer):
-            @pl.when((code >> 6) == c)
+    @pl.when(core[0] == 0)
+    def _():
+        fetch_all((keys, peer_keys))
+
+    @pl.when(core[0] == 1)
+    def _():
+        fetch_all((peer_vals, vals))
+
+    def give(dest):
+        return pltpu.make_async_copy(stage.at[dest], out.at[dest], given.at[dest])
+
+    def pass_on(dest, carry):
+        for unit in range(units):
+
+            @pl.when(codes[dest, 0, first + unit] >= 0)
             def _():
-                take(own, code, place).start()
-
-            @pl.when((code >> 6) != c)
-            def _():
-                take(peer, code, place).start()
-
-        @pl.when(core[0] == c)
-        def _():
-            each(fetch)
-
-    def pass_on(code, place):
-        take(keys, code, place).wait()
-        give(place).start()
-
-    each(pass_on)
-    each(lambda code, place: give(place).wait())
+                tile = stage.at[dest, unit]
+                pltpu.make_async_copy(tile, tile, taken.at[dest, unit]).wait()
+
+        give(dest).start()
+        return carry
+
+    def settle(dest, carry):
+        give(dest).wait()
+        return carry
+
+    lax.fori_loop(0, members, pass_on, 0)
+    lax.fori_loop(0, members, settle, 0)
 
 
 def gather_tiles(codes, core, keys, vals, peer_keys, peer_vals, first, units):
-    count = codes.shape[0] * units
+    members = codes.shape[0]
     return pl.pallas_call(
         functools.partial(gather_kernel, first, units),
-        out_shape=jax.ShapeDtypeStruct((count, BLK, DH), BF16),
-        in_specs=[SMEM, SMEM, ANY, ANY, ANY, ANY],
-        out_specs=ANY,
+        out_shape=jax.ShapeDtypeStruct((members, units, BLK, DH), BF16),
+        in_specs=[SMEM, SMEM, HBM, HBM, HBM, HBM],
+        out_specs=HBM,
         scratch_shapes=[
-            pltpu.VMEM((count, BLK, DH), BF16),
-            pltpu.SemaphoreType.DMA((count,)),
-            pltpu.SemaphoreType.DMA((count,)),
+            pltpu.VMEM((members, units, BLK, DH), BF16),
+            pltpu.SemaphoreType.DMA((members, units)),
+            pltpu.SemaphoreType.DMA((members,)),
         ],
         name="gather_tiles",
     )(codes, core, keys, vals, peer_keys, peer_vals)
@@ -163,8 +174,14 @@
     )(gk, gv, back)
 
 
-def memory_kernel(units, heads, top, scale, slots, tiles, q, gm, lq, out, kbuf, vbuf, sems):
+def memory_kernel(
+    units, heads, top, scale, slots, tiles, q, gm, lq, out, kbuf, vbuf, qbuf, gbuf, lbuf, obuf, sems, ends
+):
     blocks = q.shape[0] // BLK
+    loads = [
+        pltpu.make_async_copy(source, target, ends.at[i])
+        for i, (source, target) in enumerate(((q, qbuf), (gm, gbuf), (lq, lbuf)))
+    ]
 
     def copies(r):
         slot = slots[r]
@@ -180,38 +197,58 @@
             one.start()
         return carry
 
-    lax.fori_loop(0, blocks * heads * top, issue, 0)
+    def store(b):
+        rows = pl.ds(b * BLK, BLK)
+        return pltpu.make_async_copy(obuf.at[rows], out.at[rows], ends.at[3 + b])
+
+    first = heads * top
+    loads[0].start()
+    lax.fori_loop(0, first, issue, 0)
+    loads[1].start()
+    loads[2].start()
+    lax.fori_loop(first, blocks * first, issue, 0)
+    for load in loads:
+        load.wait()
     for b in range(blocks):
         rows = slice(b * BLK, (b + 1) * BLK)
         for r in range(b * heads * top, (b + 1) * heads * top):
             for one in copies(r):
                 one.wait()
-        for h in range(heads):
-            cols = slice(h * DH, (h + 1) * DH)
-            keys = kbuf[b * heads + h]
-            scores = dot_nt(q[rows, cols], keys)
-            peak = jnp.max(scores, axis=-1, keepdims=True)
-            expo = jnp.exp2((scores - peak) * (scale * LOG2E))
-            inverse = 1.0 / jnp.sum(expo, axis=-1, keepdims=True)
-            dprobs = dot_nt(gm[rows, cols], vbuf[b * heads + h])
-            delta = jnp.sum(expo * dprobs, axis=-1, keepdims=True) * inverse
-            dscores = (expo * (dprobs - delta)).astype(BF16)
-            grad = dot_nn(dscores, keys) * (inverse * scale)
-            out[rows, cols] = (grad + lq[rows, cols]).astype(BF16)
+        span = range(heads)
+        cols = [slice(h * DH, (h + 1) * DH) for h in span]
+        keys = [kbuf[b * heads + h] for h in span]
+        scores = [dot_nt(qbuf[rows, cols[h]], keys[h]) for h in span]
+        dprobs = [dot_nt(gbuf[rows, cols[h]], vbuf[b * heads + h]) for h in span]
+        expo = [jnp.exp2((x - jnp.max(x, axis=-1, keepdims=True)) * (scale * LOG2E)) for x in scores]
+        inverse = [1.0 / jnp.sum(x, axis=-1, keepdims=True) for x in expo]
+        delta = [jnp.sum(expo[h] * dprobs[h], axis=-1, keepdims=True) * inverse[h] for h in span]
+        dscores = [(expo[h] * (dprobs[h] - delta[h])).astype(BF16) for h in span]
+        for h in span:
+            grad = dot_nn(dscores[h], keys[h]) * (inverse[h] * scale)
+            obuf[rows, cols[h]] = (grad + lbuf[rows, cols[h]]).astype(BF16)
+        store(b).start()
+    for b in range(blocks):
+        store(b).wait()
 
 
 def memory_part(slots, tiles, q, gm, lq, units, heads, top, scale):
     tokens, width = q.shape
-    groups = tokens // BLK * heads
+    blocks = tokens // BLK
+    groups = blocks * heads
     return pl.pallas_call(
         functools.partial(memory_kernel, units, heads, top, scale),
         out_shape=jax.ShapeDtypeStruct((tokens, width), BF16),
-        in_specs=[SMEM, ANY, VMEM, VMEM, VMEM],
-        out_specs=VMEM,
+        in_specs=[SMEM, ANY, ANY, ANY, ANY],
+        out_specs=ANY,
         scratch_shapes=[
             pltpu.VMEM((groups, top * BLK, DH), BF16),
             pltpu.VMEM((groups, top * BLK, DH), BF16),
+            pltpu.VMEM((tokens, width), BF16),
+            pltpu.VMEM((tokens, width), BF16),
+            pltpu.VMEM((tokens, width), F32),
+            pltpu.VMEM((tokens, width), BF16),
             pltpu.SemaphoreType.DMA((2 * groups * top,)),
+            pltpu.SemaphoreType.DMA((3 + blocks,)),
         ],
         cost_estimate=pl.CostEstimate(
             flops=6 * groups * BLK * top * BLK * DH, transcendentals=groups * BLK * top * BLK, bytes_accessed=5 << 20
@@ -220,22 +257,47 @@
     )(slots, tiles, q, gm, lq)
 
 
-def join_kernel(*refs):
-    *parts, out = refs
-    rows = parts[0].shape[0]
-    for i, part in enumerate(parts):
-        out[i * rows : (i + 1) * rows] = part[...]
-
-
-def join(parts):
-    rows, width = parts[0].shape
-    return pl.pallas_call(
-        join_kernel,
-        out_shape=jax.ShapeDtypeStruct((rows * len(parts), width), parts[0].dtype),
-        in_specs=[VMEM] * len(parts),
-        out_specs=VMEM,
+def join_kernel(pieces, *refs):
+    outs = 1 + max(piece[0] for piece in pieces)
+    sources, targets, stages, (taken, given) = (
+        refs[: -2 * outs - 2],
+        refs[-2 * outs - 2 : -outs - 2],
+        refs[-outs - 2 : -2],
+        refs[-2:],
+    )
+    count = [0] * outs
+    steps = []
+    for i, (out, source, row) in enumerate(pieces):
+        rows = stages[out].shape[0] // sum(piece[0] == out for piece in pieces)
+        here = pl.ds(count[out] * rows, rows)
+        count[out] += 1
+        steps.append(
+            (
+                pltpu.make_async_copy(sources[source].at[pl.ds(row, rows)], stages[out].at[here], taken.at[i]),
+                pltpu.make_async_copy(stages[out].at[here], targets[out].at[here], given.at[i]),
+            )
+        )
+    for take, _ in steps:
+        take.start()
+    for take, give in steps:
+        take.wait()
+        give.start()
+    for _, give in steps:
+        give.wait()
+
+
+def join(pieces, sources, rows):
+    width = sources[0].shape[1]
+    shapes = [(n, width) for n in rows]
+    return pl.pallas_call(
+        functools.partial(join_kernel, tuple(pieces)),
+        out_shape=tuple(jax.ShapeDtypeStruct(shape, BF16) for shape in shapes),
+        in_specs=[HBM] * len(sources),
+        out_specs=(HBM,) * len(rows),
+        scratch_shapes=[pltpu.VMEM(shape, BF16) for shape in shapes]
+        + [pltpu.SemaphoreType.DMA((len(pieces),)), pltpu.SemaphoreType.DMA((len(pieces),))],
         name="join",
-    )(*parts)
+    )(*sources)
 
 
 def head_kernel(order, go_a, go_b, w_a, w_b, out):
@@ -277,12 +339,13 @@
     )(order, grad_out, grad_out, w_a, w_b)
 
 
-def local_kernel(scale, window, start, gate, q, k, v, halo, hg, gm_out, lq_out, gk_out, gv_out, back_out):
+def local_kernel(scale, window, start, gate, q, k, v, hk, hv, hg, gm_out, lq_out, gk_out, gv_out, back_out):
     head = pl.program_id(0)
     share = gate[head]
     blocks = q.shape[0] // BLK
-    key_blocks = [halo[0, :BLK], halo[0, BLK:]] + [k[i * BLK : (i + 1) * BLK] for i in range(blocks)]
-    val_blocks = [halo[1, :BLK], halo[1, BLK:]] + [v[i * BLK : (i + 1) * BLK] for i in range(blocks)]
+    tail = q.shape[0] - 2 * BLK
+    key_blocks = [hk[tail : tail + BLK], hk[tail + BLK :]] + [k[i * BLK : (i + 1) * BLK] for i in range(blocks)]
+    val_blocks = [hv[tail : tail + BLK], hv[tail + BLK :]] + [v[i * BLK : (i + 1) * BLK] for i in range(blocks)]
     key_sums = [None] * (blocks + 2)
     val_sums = [None] * (blocks + 2)
     row = lax.broadcasted_iota(jnp.int32, (BLK, 3 * BLK), 0)
@@ -318,7 +381,7 @@
         gv_out[i * BLK : (i + 1) * BLK, :] = val_sums[i + 2]
 
 
-def local_part(window, start, gate, q, k, v, halo, hg, scale):
+def local_part(window, start, gate, q, k, v, hk, hv, hg, scale):
     tokens, width = q.shape
     heads = width // DH
     column = pl.BlockSpec((tokens, DH), lambda h: (0, h))
@@ -333,13 +396,13 @@
             jax.ShapeDtypeStruct((tokens, width), F32),
             jax.ShapeDtypeStruct((2, 2 * BLK, width), BF16),
         ),
-        in_specs=[SMEM, SMEM, SMEM, column, column, column, pair, column],
+        in_specs=[SMEM, SMEM, SMEM, column, column, column, column, column, column],
         out_specs=(column, column, column, column, pair),
         cost_estimate=pl.CostEstimate(
             flops=10 * tokens * 3 * BLK * width, transcendentals=tokens * 3 * BLK * heads, bytes_accessed=6 << 20
         ),
         name="local_part",
-    )(window, start, gate, q, k, v, halo, hg)
+    )(window, start, gate, q, k, v, hk, hv, hg)
 
 
 def place_of(x, y, core):
@@ -384,6 +447,10 @@
     scale = 1.0 / math.sqrt(DH)
     tokens = queries.shape[0]
 
+    onward = [(i, (i + 1) % members) for i in range(members)]
+    halo_keys = lax.ppermute(local_keys, "mem", onward)
+    halo_values = lax.ppermute(local_values, "mem", onward)
+
     request, slots = requests(tile_ids, members)
     codes = lax.all_to_all(request, "mem", split_axis=0, concat_axis=0, tiled=True)
 
@@ -392,20 +459,18 @@
     peer_vals = lax.ppermute(memory_values, "mem", partner)
     rows = [out_weight] + [lax.ppermute(out_weight, "mem", torus(shift, 0)) for shift in (1, 2, 3)]
     sources = (codes, core, memory_keys, memory_values, peer_keys, peer_vals)
-    sent = gather_tiles(*sources, 0, UNITS).reshape(members, UNITS, BLK, DH)
-    band = join(rows)
+    sent = gather_tiles(*sources, 0, UNITS)
+    (band,) = join([(0, i, 0) for i in range(4)], rows, (4 * out_weight.shape[0],))
     bands = [band] + [lax.ppermute(band, "mem", torus(shift, 1)) for shift in (1, 2, 3)]
-    halo = jnp.stack([local_keys[tokens - 2 * BLK :], local_values[tokens - 2 * BLK :]])
-    halo = lax.ppermute(halo, "mem", [(i, i + 1) for i in range(members - 1)])
     tiles = lax.all_to_all(sent, "mem", split_axis=0, concat_axis=0, tiled=True)
 
-    w_own = join(bands)
+    (w_own,) = join([(0, i, 0) for i in range(4)], bands, (4 * band.shape[0],))
     w_peer = lax.ppermute(w_own, "mem", partner)
     head_grad = head_part(arrival(me), grad_out, w_own, w_peer)
     gate = jax.nn.sigmoid(gate_logits)
     start = (me * tokens).reshape(1)
     gm, lq, gk, gv, back = local_part(
-        window, start, gate, queries, local_keys, local_values, halo, head_grad, scale
+        window, start, gate, queries, local_keys, local_values, halo_keys, halo_values, head_grad, scale
     )
     back = lax.ppermute(back, "mem", [(i + 1, i) for i in range(members - 1)])
     grad_keys, grad_values = closing(gk, gv, back)
@@ -415,7 +480,7 @@
         return memory_part(slots, flat, queries, gm, lq, UNITS, heads, top, scale)
 
     def with_sixth():
-        sixth = gather_tiles(*sources, UNITS, 1).reshape(members, 1, BLK, DH)
+        sixth = gather_tiles(*sources, UNITS, 1)
         sixth = lax.all_to_all(sixth, "mem", split_axis=0, concat_axis=0, tiled=True)
         flat = jnp.concatenate([tiles, sixth], axis=1).reshape(members * (UNITS + 1), BLK, DH)
         return memory_part(slots, flat, queries, gm, lq, UNITS + 1, heads, top, scale)

time: 179 us -> 176 us (0.983)
  Pallas kernels: 48 us -> 43.9 us
    pallas_call x1, Pallas kernels: 8.62 us -> 6.23 us  [memory_part(): pl.pallas_call(functools.partial(memory_kernel, units, heads, top, scale)...]
  transfers between devices with their start and end apart: 13 -> 14, of which waited for: 6 -> 7; matrix products, arithmetic and copies ran while one was open for 1% -> 1% of each run, Pallas kernels for 18% -> 18%
where the time goes in v2:
time: 176 us; the launch traced here: 175 us
  waiting for transfers between devices  88.9 us (51%)
  Pallas kernels  43.9 us (25%)
  starting transfers between devices  35.2 us (20%)
  local copies, waits for them, and re-layouts  3.62 us (2%)
  other arithmetic  1.87 us (1%)
    ppermute x3, waiting for transfers between devices, body(): lax.ppermute(out_weight, 'mem', torus(shift, 0))  59 us
    ppermute x3, waiting for transfers between devices, body(): lax.ppermute(band, 'mem', torus(shift, 1))  14.7 us
    pallas_call x1, Pallas kernels, head_part(): pl.pallas_call(head_kernel, grid_spec=pltpu.PrefetchScalarGridSpec(num_sc...  13.4 us
    pallas_call x1, Pallas kernels, local_part(): pl.pallas_call(functools.partial(local_kernel, scale), grid=(heads,), out...  9.01 us
    ppermute x1, starting transfers between devices, body(): w_peer = lax.ppermute(w_own, 'mem', partner)  7.67 us
    ppermute x1, waiting for transfers between devices, body(): back = lax.ppermute(back, 'mem', [(i + 1, i) for i in range(members - 1)])  7.42 us
    all_to_all x1, waiting for transfers between devices, body(): lax.all_to_all(request, 'mem', split_axis=0, concat_axis=0, tiled=True)  6.89 us
    pallas_call x1, Pallas kernels, memory_part(): pl.pallas_call(functools.partial(memory_kernel, units, heads, top, scale)...  6.23 us
  transfers between devices with their start and end apart: 14, of which 7 were waited for; matrix products, arithmetic and copies ran while one was open for 1% of the time, Pallas kernels for 18%

profile of v2, /device:TPU:1, one launch (start us, length us, event | category | flops | bytes accessed | tf_op | source)
XLA Modules:
  0.0 175.2 jit_solution(13397321238865739595)
XLA Ops:
  0.6 3.3 %collective-permute-start = (bf16[2048,512]{1,0:T(8,128)(2,1)}, bf16[2048,512]{1,0:T(8,128)(2,1)S(1)}, u32[]{:S(2)}, u32[]{:S(2)}) collective-permute-start(bf16[2048,512]{1,0:T(8,128)(2,1)} %keys.1), channel_id=1, source_target_pairs={{0,8},{8,0},{16,24},{24,16},{32,40},{40,32},{48,56},{56,48},{64,72... | collective-permute-start | bytes 6291464 | tf_op jit(solution)/shard_map/ppermute | solution.py:458
  3.9 0.1 collective-permute-start.1
  4.0 2.7 %requests.1 = (s32[32,1,128]{2,1,0:T(1,128)}, s32[48]{0:T(128)S(1)}) custom-call(s32[3,4,4]{2,1,0:T(4,128)} %ids.1), custom_call_target="tpu_custom_call" | custom-call | tf_op jit(solution)/shard_map/requests/pallas_call | solution.py:78
  6.7 5.8 %all-to-all-start.1 = ((s32[32,1,128]{2,1,0:T(1,128)}), s32[32,1,128]{2,1,0:T(1,128)S(1)}, u32[]{:S(2)}, u32[]{:S(2)}) async-start(s32[32,1,128]{2,1,0:T(1,128)} %get-tuple-element.63), calls=%async_computation.1 | async-start | bytes 32768 | tf_op jit(solution)/shard_map/all_to_all | solution.py:455
  12.5 6.9 %all-to-all-done.1.codes = s32[32,1,128]{2,1,0:T(1,128)S(1)} async-done(((s32[32,1,128]{2,1,0:T(1,128)}), s32[32,1,128]{2,1,0:T(1,128)S(1)}, u32[]{:S(2)}, u32[]{:S(2)}) %all-to-all-start.1) | async-done | bytes 16416 | tf_op jit(solution)/shard_map/all_to_all | solution.py:455
  19.4 0.0 collective-permute-done.peer_keys
  19.4 0.0 collective-permute-done.1.peer_vals
  19.4 5.9 %gather_tiles.3 = bf16[32,5,128,128]{3,2,1,0:T(8,128)(2,1)} custom-call(s32[32,1,128]{2,1,0:T(1,128)S(1)} %all-to-all-done.1.codes, s32[1]{0:T(128)} %bitcast.2.core, bf16[2048,512]{1,0:T(8,128)(2,1)} %keys.1, bf16[2048,512]{1,0:T(8,128)(2,1)} %vals.1, bf16[2048,512]{1,0:T(8,128)(2,1)S(1)} %collective-permute-done.peer_keys, ...), custom_call_target="tpu_custom_call" | custom-call | tf_op jit(solution)/shard_map/gather_tiles/pallas_call | solution.py:146
  25.4 0.0 copy-start.7
  25.4 6.0 %all-to-all-start.2 = ((bf16[32,5,128,128]{3,2,1,0:T(8,128)(2,1)}), bf16[32,5,128,128]{3,2,1,0:T(8,128)(2,1)}, u32[]{:S(2)}, u32[]{:S(2)}) async-start(bf16[32,5,128,128]{3,2,1,0:T(8,128)(2,1)} %gather_tiles.3), calls=%async_computation.2 | async-start | bytes 10485760 | tf_op jit(solution)/shard_map/all_to_all | solution.py:465
  31.4 0.0 copy-start.13
  31.4 3.0 %collective-permute-start.5 = (bf16[128,512]{1,0:T(8,128)(2,1)S(1)}, bf16[128,512]{1,0:T(8,128)(2,1)S(1)}, u32[]{:S(2)}, u32[]{:S(2)}) collective-permute-start(bf16[128,512]{1,0:T(8,128)(2,1)S(1)} %copy-done.7), channel_id=1, source_target_pairs={{0,128},{8,40},{16,144},{24,56},{32,160},{40,8},{48,176},{56,24},{... | collective-permute-start | bytes 393224 | tf_op jit(solution)/shard_map/ppermute | solution.py:460
  34.4 0.3 collective-permute-start.4
  34.7 2.4 %collective-permute-start.6 = (bf16[128,512]{1,0:T(8,128)(2,1)S(1)}, bf16[128,512]{1,0:T(8,128)(2,1)S(1)}, u32[]{:S(2)}, u32[]{:S(2)}) collective-permute-start(bf16[128,512]{1,0:T(8,128)(2,1)S(1)} %copy-done.7), channel_id=1, source_target_pairs={{0,192},{8,56},{16,208},{24,8},{32,224},{40,24},{48,240},{56,40},{... | collective-permute-start | bytes 393224 | tf_op jit(solution)/shard_map/ppermute | solution.py:460
  37.1 57.6 %collective-permute-done.5.refs_2_ = bf16[128,512]{1,0:T(8,128)(2,1)S(1)} collective-permute-done((bf16[128,512]{1,0:T(8,128)(2,1)S(1)}, bf16[128,512]{1,0:T(8,128)(2,1)S(1)}, u32[]{:S(2)}, u32[]{:S(2)}) %collective-permute-start.5) | collective-permute-done | bytes 131104 | tf_op jit(solution)/shard_map/ppermute | solution.py:460
  94.7 1.4 collective-permute-done.4.refs_1_
  96.1 0.0 collective-permute-done.6.refs_3_
  96.1 0.6 copy-done.9
  96.7 0.7 copy-done.10
  97.4 1.8 %join.2.refs_0_ = bf16[512,512]{1,0:T(8,128)(2,1)} custom-call(bf16[128,512]{1,0:T(8,128)(2,1)} %refs_0_.1, bf16[128,512]{1,0:T(8,128)(2,1)} %copy-done.9, bf16[128,512]{1,0:T(8,128)(2,1)} %copy-done.8, bf16[128,512]{1,0:T(8,128)(2,1)} %copy-done.10), custom_call_target="tpu_custom_call" | custom-call | tf_op jit(solution)/shard_map/join/pallas_call | solution.py:292
  99.2 1.6 collective-permute-start.9
  100.8 0.0 collective-permute-start.8
  100.8 0.7 collective-permute-start.7
  101.5 11.4 %collective-permute-done.9.refs_3_ = bf16[512,512]{1,0:T(8,128)(2,1)S(1)} collective-permute-done((bf16[512,512]{1,0:T(8,128)(2,1)}, bf16[512,512]{1,0:T(8,128)(2,1)S(1)}, u32[]{:S(2)}, u32[]{:S(2)}) %collective-permute-start.9) | collective-permute-done | bytes 524320 | tf_op jit(solution)/shard_map/ppermute | solution.py:464
  112.9 0.0 collective-permute-done.8.refs_2_
  112.9 3.3 %collective-permute-done.7.refs_1_ = bf16[512,512]{1,0:T(8,128)(2,1)S(1)} collective-permute-done((bf16[512,512]{1,0:T(8,128)(2,1)}, bf16[512,512]{1,0:T(8,128)(2,1)S(1)}, u32[]{:S(2)}, u32[]{:S(2)}) %collective-permute-start.7) | collective-permute-done | bytes 524320 | tf_op jit(solution)/shard_map/ppermute | solution.py:464
  116.2 0.0 copy-done.5
  116.2 0.8 copy-done.6
  117.0 2.4 %join.3.w_a = bf16[2048,512]{1,0:T(8,128)(2,1)} custom-call(bf16[512,512]{1,0:T(8,128)(2,1)} %join.2.refs_0_, bf16[512,512]{1,0:T(8,128)(2,1)} %copy-done.6, bf16[512,512]{1,0:T(8,128)(2,1)} %copy-done.5, bf16[512,512]{1,0:T(8,128)(2,1)} %copy-done.4), custom_call_target="tpu_custom_call" | custom-call | tf_op jit(solution)/shard_map/join/pallas_call | solution.py:292
  119.4 7.7 %collective-permute-start.10 = (bf16[2048,512]{1,0:T(8,128)(2,1)}, bf16[2048,512]{1,0:T(8,128)(2,1)}, u32[]{:S(2)}, u32[]{:S(2)}) collective-permute-start(bf16[2048,512]{1,0:T(8,128)(2,1)} %join.3.w_a), channel_id=1, source_target_pairs={{0,8},{8,0},{16,24},{24,16},{32,40},{40,32},{48,56},{56,48},{64,72... | collective-permute-start | bytes 6291464 | tf_op jit(solution)/shard_map/ppermute | solution.py:468
  127.1 1.7 collective-permute-start.2
  128.8 0.4 collective-permute-start.3
  129.3 0.6 add_select_fusion.order
  129.8 0.5 add_divide_fusion.gate
  130.4 0.8 collective-permute-done.10.w_b
  131.2 13.4 %head_part.1.hg = f32[384,512]{1,0:T(8,128)} custom-call(s32[2,16]{1,0:T(2,128)} %add_select_fusion.order, bf16[384,4096]{1,0:T(8,128)(2,1)} %go_b.1, bf16[384,4096]{1,0:T(8,128)(2,1)} %go_b.1, bf16[2048,512]{1,0:T(8,128)(2,1)} %join.3.w_a, bf16[2048,512]{1,0:T(8,128)(2,1)} %collective-permute-done.10.w_b), custom_call_target="tpu_custom_call" | custom-call | flops 1610612736 | bytes 9437184 | tf_op jit(solution)/shard_map/head_part/pallas_call | solution.py:321
  144.6 0.0 collective-permute-done.2.hk
  144.6 0.0 collective-permute-done.3.hv
  144.6 0.7 copy-done.11
  145.4 0.7 copy-done.12
  146.1 9.0 %local_part.1 = (bf16[384,512]{1,0:T(8,128)(2,1)}, f32[384,512]{1,0:T(8,128)S(1)}, f32[384,512]{1,0:T(8,128)}, f32[384,512]{1,0:T(8,128)}, bf16[2,256,512]{2,1,0:T(8,128)(2,1)}) custom-call(s32[3]{0:T(128)} %window.1, s32[1]{0:T(128)} %bitcast.3.start, f32[4]{0:T(128)} %add_divide_fusion.gate, bf16[384,512]{1,0:T(8,128)(2,1)S(1)} %copy-done.2, ...), custom_call_target="tpu_custom_call" | custom-call | flops 754974720 | bytes 6291456 | tf_op jit(solution)/shard_map/local_part/pallas_call | solution.py:389
  155.1 2.3 %collective-permute-start.11 = (bf16[2,256,512]{2,1,0:T(8,128)(2,1)}, bf16[2,256,512]{2,1,0:T(8,128)(2,1)}, u32[]{:S(2)}, u32[]{:S(2)}) collective-permute-start(bf16[2,256,512]{2,1,0:T(8,128)(2,1)} %get-tuple-element.69), channel_id=1, source_target_pairs={{8,0},{16,8},{24,16},{32,24},{40,32},{48,40},{56,48},{64,56},{72,6... | collective-permute-start | bytes 1572872 | tf_op jit(solution)/shard_map/ppermute | solution.py:475
  157.4 0.7 slice_reduce_fusion
  158.8 7.4 %collective-permute-done.11.back = bf16[2,256,512]{2,1,0:T(8,128)(2,1)} collective-permute-done((bf16[2,256,512]{2,1,0:T(8,128)(2,1)}, bf16[2,256,512]{2,1,0:T(8,128)(2,1)}, u32[]{:S(2)}, u32[]{:S(2)}) %collective-permute-start.11) | collective-permute-done | bytes 524320 | tf_op jit(solution)/shard_map/ppermute | solution.py:475
  166.2 2.5 %closing.1 = (bf16[384,512]{1,0:T(8,128)(2,1)}, bf16[384,512]{1,0:T(8,128)(2,1)}) custom-call(f32[384,512]{1,0:T(8,128)} %get-tuple-element.67.gk, f32[384,512]{1,0:T(8,128)} %get-tuple-element.68.gv, bf16[2,256,512]{2,1,0:T(8,128)(2,1)} %collective-permute-done.11.back), custom_call_target="tpu_custom_call" | custom-call | tf_op jit(solution)/shard_map/closing/pallas_call | solution.py:168
  168.7 0.0 all-to-all-done.2
  168.7 6.4 %conditional.1 = (bf16[384,512]{1,0:T(8,128)(2,1)}) conditional(s32[]{:T(128)} %convert_element_type.3, (bf16[32,5,128,128]{3,2,1,0:T(8,128)(2,1)}, s32[48]{0:T(128)S(1)}, bf16[384,512]{1,0:T(8,128)(2,1)S(1)}, bf16[384,512]{1,0:T(8,128)(2,1)}, f32[384,512]{1,0:T(8,128)S(1)}) %tuple.22, (s32[32,1,128]{2,1,0:T(1,128)S(1)}, s32[1]{0:T(128)}, ...), branch_computations={%region_1.2_spmd, %region_2.3_spmd} | conditional | flops 607125504 | bytes 21495844 | solution.py:488
  168.8 6.2 %memory_part.2 = bf16[384,512]{1,0:T(8,128)(2,1)} custom-call(s32[48]{0:T(128)S(1)} %get-tuple-element.20.slots, bf16[160,128,128]{2,1,0:T(8,128)(2,1)} %bitcast.tiles, bf16[384,512]{1,0:T(8,128)(2,1)S(1)} %get-tuple-element.37.q, bf16[384,512]{1,0:T(8,128)(2,1)} %get-tuple-element.38.gm, f32[384,512]{1,0:T(8,128)S(1)} %get-tuple-element.39.lq), custom_call_target="tpu_custom_call" | custom-call | flops 603979776 | bytes 5242880 | tf_op jit(solution)/shard_map/cond/branch_0_fun/memory_part/pallas_call | solution.py:238
  (19 shorter events, 0.0 us)
Async XLA Ops:
  0.6 18.8 %collective-permute-start = (bf16[2048,512]{1,0:T(8,128)(2,1)}, bf16[2048,512]{1,0:T(8,128)(2,1)S(1)}, u32[]{:S(2)}, u32[]{:S(2)}) collective-permute-start(bf16[2048,512]{1,0:T(8,128)(2,1)} %keys.1), channel_id=1, source_target_pairs={{0,8},{8,0},{16,24},{24,16},{32,40},{40,32},{48,56},{56,48},{64,72... | collective-permute-start | bytes 6291464 | tf_op jit(solution)/shard_map/ppermute | solution.py:458
  3.9 15.5 %collective-permute-start.1 = (bf16[2048,512]{1,0:T(8,128)(2,1)}, bf16[2048,512]{1,0:T(8,128)(2,1)}, u32[]{:S(2)}, u32[]{:S(2)}) collective-permute-start(bf16[2048,512]{1,0:T(8,128)(2,1)} %vals.1), channel_id=1, source_target_pairs={{0,8},{8,0},{16,24},{24,16},{32,40},{40,32},{48,56},{56,48},{64,72... | collective-permute-start | bytes 6291464 | tf_op jit(solution)/shard_map/ppermute | solution.py:459
  6.7 12.7 %all-to-all-start.1 = ((s32[32,1,128]{2,1,0:T(1,128)}), s32[32,1,128]{2,1,0:T(1,128)S(1)}, u32[]{:S(2)}, u32[]{:S(2)}) async-start(s32[32,1,128]{2,1,0:T(1,128)} %get-tuple-element.63), calls=%async_computation.1 | async-start | bytes 32768 | tf_op jit(solution)/shard_map/all_to_all | solution.py:455
  19.4 6.0 %copy-start.1 = (bf16[2048,512]{1,0:T(8,128)(2,1)}, bf16[2048,512]{1,0:T(8,128)(2,1)S(1)}, u32[]{:S(2)}) copy-start(bf16[2048,512]{1,0:T(8,128)(2,1)S(1)} %collective-permute-done.peer_keys) | copy-start | bytes 6291460
  25.4 6.0 %copy-start.7 = (bf16[128,512]{1,0:T(8,128)(2,1)S(1)}, bf16[128,512]{1,0:T(8,128)(2,1)}, u32[]{:S(2)}) copy-start(bf16[128,512]{1,0:T(8,128)(2,1)} %refs_0_.1) | copy-start | bytes 393220
  25.4 143.3 %all-to-all-start.2 = ((bf16[32,5,128,128]{3,2,1,0:T(8,128)(2,1)}), bf16[32,5,128,128]{3,2,1,0:T(8,128)(2,1)}, u32[]{:S(2)}, u32[]{:S(2)}) async-start(bf16[32,5,128,128]{3,2,1,0:T(8,128)(2,1)} %gather_tiles.3), calls=%async_computation.2 | async-start | bytes 10485760 | tf_op jit(solution)/shard_map/all_to_all | solution.py:465
  31.4 98.4 %copy-start.13 = (f32[4]{0:T(128)S(1)}, f32[4]{0:T(128)}, u32[]{:S(2)}) copy-start(f32[4]{0:T(128)} %param.19) | copy-start | bytes 52
  31.4 63.3 %collective-permute-start.5 = (bf16[128,512]{1,0:T(8,128)(2,1)S(1)}, bf16[128,512]{1,0:T(8,128)(2,1)S(1)}, u32[]{:S(2)}, u32[]{:S(2)}) collective-permute-start(bf16[128,512]{1,0:T(8,128)(2,1)S(1)} %copy-done.7), channel_id=1, source_target_pairs={{0,128},{8,40},{16,144},{24,56},{32,160},{40,8},{48,176},{56,24},{... | collective-permute-start | bytes 393224 | tf_op jit(solution)/shard_map/ppermute | solution.py:460
  34.4 61.7 %collective-permute-start.4 = (bf16[128,512]{1,0:T(8,128)(2,1)S(1)}, bf16[128,512]{1,0:T(8,128)(2,1)S(1)}, u32[]{:S(2)}, u32[]{:S(2)}) collective-permute-start(bf16[128,512]{1,0:T(8,128)(2,1)S(1)} %copy-done.7), channel_id=1, source_target_pairs={{0,64},{8,24},{16,80},{24,40},{32,96},{40,56},{48,112},{56,8},{64,... | collective-permute-start | bytes 393224 | tf_op jit(solution)/shard_map/ppermute | solution.py:460
  34.7 61.4 %collective-permute-start.6 = (bf16[128,512]{1,0:T(8,128)(2,1)S(1)}, bf16[128,512]{1,0:T(8,128)(2,1)S(1)}, u32[]{:S(2)}, u32[]{:S(2)}) collective-permute-start(bf16[128,512]{1,0:T(8,128)(2,1)S(1)} %copy-done.7), channel_id=1, source_target_pairs={{0,192},{8,56},{16,208},{24,8},{32,224},{40,24},{48,240},{56,40},{... | collective-permute-start | bytes 393224 | tf_op jit(solution)/shard_map/ppermute | solution.py:460
  94.7 1.4 copy-start.8
  96.1 0.7 copy-start.9
  96.7 0.7 copy-start.10
  99.2 13.7 %collective-permute-start.9 = (bf16[512,512]{1,0:T(8,128)(2,1)}, bf16[512,512]{1,0:T(8,128)(2,1)S(1)}, u32[]{:S(2)}, u32[]{:S(2)}) collective-permute-start(bf16[512,512]{1,0:T(8,128)(2,1)} %join.2.refs_0_), channel_id=1, source_target_pairs={{0,48},{8,200},{16,0},{24,216},{32,16},{40,232},{48,32},{56,248},{... | collective-permute-start | bytes 1572872 | tf_op jit(solution)/shard_map/ppermute | solution.py:464
  100.8 12.1 %collective-permute-start.8 = (bf16[512,512]{1,0:T(8,128)(2,1)}, bf16[512,512]{1,0:T(8,128)(2,1)S(1)}, u32[]{:S(2)}, u32[]{:S(2)}) collective-permute-start(bf16[512,512]{1,0:T(8,128)(2,1)} %join.2.refs_0_), channel_id=1, source_target_pairs={{0,32},{8,136},{16,48},{24,152},{32,0},{40,168},{48,16},{56,184},{... | collective-permute-start | bytes 1572872 | tf_op jit(solution)/shard_map/ppermute | solution.py:464
  100.8 15.4 %collective-permute-start.7 = (bf16[512,512]{1,0:T(8,128)(2,1)}, bf16[512,512]{1,0:T(8,128)(2,1)S(1)}, u32[]{:S(2)}, u32[]{:S(2)}) collective-permute-start(bf16[512,512]{1,0:T(8,128)(2,1)} %join.2.refs_0_), channel_id=1, source_target_pairs={{0,16},{8,72},{16,32},{24,88},{32,48},{40,104},{48,0},{56,120},{64... | collective-permute-start | bytes 1572872 | tf_op jit(solution)/shard_map/ppermute | solution.py:464
  112.9 3.3 %copy-start.4 = (bf16[512,512]{1,0:T(8,128)(2,1)}, bf16[512,512]{1,0:T(8,128)(2,1)S(1)}, u32[]{:S(2)}) copy-start(bf16[512,512]{1,0:T(8,128)(2,1)S(1)} %collective-permute-done.9.refs_3_) | copy-start | bytes 1572868
  112.9 3.3 %copy-start.5 = (bf16[512,512]{1,0:T(8,128)(2,1)}, bf16[512,512]{1,0:T(8,128)(2,1)S(1)}, u32[]{:S(2)}) copy-start(bf16[512,512]{1,0:T(8,128)(2,1)S(1)} %collective-permute-done.8.refs_2_) | copy-start | bytes 1572868
  116.2 0.8 copy-start.6
  119.4 11.8 %collective-permute-start.10 = (bf16[2048,512]{1,0:T(8,128)(2,1)}, bf16[2048,512]{1,0:T(8,128)(2,1)}, u32[]{:S(2)}, u32[]{:S(2)}) collective-permute-start(bf16[2048,512]{1,0:T(8,128)(2,1)} %join.3.w_a), channel_id=1, source_target_pairs={{0,8},{8,0},{16,24},{24,16},{32,40},{40,32},{48,56},{56,48},{64,72... | collective-permute-start | bytes 6291464 | tf_op jit(solution)/shard_map/ppermute | solution.py:468
  127.1 17.5 %collective-permute-start.2 = (bf16[384,512]{1,0:T(8,128)(2,1)}, bf16[384,512]{1,0:T(8,128)(2,1)S(1)}, u32[]{:S(2)}, u32[]{:S(2)}) collective-permute-start(bf16[384,512]{1,0:T(8,128)(2,1)} %k.1), channel_id=1, source_target_pairs={{0,8},{8,16},{16,24},{24,32},{32,40},{40,48},{48,56},{56,64},{64,7... | collective-permute-start | bytes 1179656 | tf_op jit(solution)/shard_map/ppermute | solution.py:451
  128.8 15.8 %collective-permute-start.3 = (bf16[384,512]{1,0:T(8,128)(2,1)}, bf16[384,512]{1,0:T(8,128)(2,1)S(1)}, u32[]{:S(2)}, u32[]{:S(2)}) collective-permute-start(bf16[384,512]{1,0:T(8,128)(2,1)} %v.1), channel_id=1, source_target_pairs={{0,8},{8,16},{16,24},{24,32},{32,40},{40,48},{48,56},{56,64},{64,7... | collective-permute-start | bytes 1179656 | tf_op jit(solution)/shard_map/ppermute | solution.py:452
  130.4 15.7 %copy-start.2 = (bf16[384,512]{1,0:T(8,128)(2,1)S(1)}, bf16[384,512]{1,0:T(8,128)(2,1)}, u32[]{:S(2)}) copy-start(bf16[384,512]{1,0:T(8,128)(2,1)} %q.1) | copy-start | bytes 1179652
  130.4 38.3 %copy-start = (bf16[2048,512]{1,0:T(8,128)(2,1)S(1)}, bf16[2048,512]{1,0:T(8,128)(2,1)}, u32[]{:S(2)}) copy-start(bf16[2048,512]{1,0:T(8,128)(2,1)} %keys.1) | copy-start | bytes 6291460
  144.6 0.7 copy-start.11
  145.4 0.7 copy-start.12
  155.1 11.1 %collective-permute-start.11 = (bf16[2,256,512]{2,1,0:T(8,128)(2,1)}, bf16[2,256,512]{2,1,0:T(8,128)(2,1)}, u32[]{:S(2)}, u32[]{:S(2)}) collective-permute-start(bf16[2,256,512]{2,1,0:T(8,128)(2,1)} %get-tuple-element.69), channel_id=1, source_target_pairs={{8,0},{16,8},{24,16},{32,24},{40,32},{48,40},{56,48},{64,56},{72,6... | collective-permute-start | bytes 1572872 | tf_op jit(solution)/shard_map/ppermute | solution.py:475
